TPU v7x, 128 devices: a whole 4x4x4 slice. The times are simulated.
128 devices in a mesh: row: 16 (over y, z_hi, core), col: 8 (over x, z_lo).
Axes of the slice: x: 4, y: 4, z: 4 (z_hi: 2, z_lo: 2; z = z_hi * 2 + z_lo), core: 2. Of those that a mesh axis runs over, the one named last changes fastest.
Arguments:
- homolog_embedding: bfloat16 [128, 1024, 64], P(('row', 'col')), may hold values from -6 to 6
- split_mapping_matrix: bfloat16 [64, 64], replicated, may hold values from -0.75 to 0.75
- couple_mapping_matrix: bfloat16 [1024, 128], replicated, may hold values from -1.5 to 1.5
- couple_offset_vector: bfloat16 [128], replicated, may hold values from -3 to 3
- incoming_adjoint_couple: bfloat16 [1024, 1024, 128], P('row', 'col'), may hold values from -0.29882812 to 0.29882812
Outputs:
- pair_delta_output: bfloat16 [1024, 1024, 128], P('row', 'col')
- alignment_gradient: bfloat16 [128, 1024, 64], P(('row', 'col'))
- out_weight_grad: float32 [1024, 128], replicated
All inputs are finite; a program needn't handle non-finite values.
Results may differ from a plain program's by a relative error of at most 0.015.
Values may be sent and summed in bfloat16 or wider, within the bound.
A program may use at most 64 MiB of HBM per device.

v0:
```python
import math

import jax
import jax.numpy as jnp
from jax import lax
from jax.sharding import PartitionSpec as P


def copy_for_each(array, axis):
    size = lax.axis_size(axis)
    return lax.all_to_all(
        jnp.broadcast_to(array[None], (size, *array.shape)), axis, 0, 0, tiled=True
    )


def laid_out(pieces, dim):
    pieces = jnp.moveaxis(pieces, 0, dim)
    shape = pieces.shape
    return pieces.reshape(*shape[:dim], shape[dim] * shape[dim + 1], *shape[dim + 2 :])


def gather_directly(array, axis, dim):
    pieces = copy_for_each(array, axis)
    return laid_out(pieces, dim)


def cut_along(array, dim, size):
    before, after = (array.shape[:dim], array.shape[dim + 1 :])
    return jnp.moveaxis(array.reshape(*before, size, -1, *after), dim, 0)


def summed_on_arrival(array, axis, dim):
    size = lax.axis_size(axis)
    pieces = lax.all_to_all(cut_along(array, dim, size), axis, 0, 0, tiled=True)
    return jnp.sum(pieces.astype(jnp.float32), axis=0)


def standardize_features(homolog_embedding):
    mapped_halves = homolog_embedding.astype(jnp.float32)
    center = jnp.mean(mapped_halves, axis=-1, keepdims=True)
    spread = jnp.mean((mapped_halves - center) * (mapped_halves - center), axis=-1, keepdims=True)
    reciprocal_spread = lax.rsqrt(spread + 1e-05)
    return ((mapped_halves - center) * reciprocal_spread, reciprocal_spread)


def regroup(mapped_halves, outer_count, inner_count):
    shaped = mapped_halves.reshape((outer_count, inner_count, -1) + mapped_halves.shape[1:])
    return jnp.swapaxes(shaped, 0, 1).reshape(mapped_halves.shape)


def on_device(
    homolog_embedding,
    split_mapping_matrix,
    couple_mapping_matrix,
    couple_offset_vector,
    incoming_adjoint_couple,
):
    rows_count = lax.axis_size("row")
    cols_count = lax.axis_size("col")
    width = split_mapping_matrix.shape[1] // 2
    standardized_activations, reciprocal_spread = standardize_features(homolog_embedding)
    normalized_input = standardized_activations.astype(jnp.bfloat16)
    factors = jnp.dot(
        normalized_input, split_mapping_matrix, preferred_element_type=jnp.float32
    ).astype(jnp.bfloat16)
    left = factors[..., :width]
    right = factors[..., width:]
    left_part = lax.all_to_all(left, "row", split_axis=1, concat_axis=0, tiled=True)
    left_panel = regroup(gather_directly(left_part, "col", 0), cols_count, rows_count)
    right_part = lax.all_to_all(right, "col", split_axis=1, concat_axis=0, tiled=True)
    right_panel = gather_directly(right_part, "row", 0)
    seq_total = left_panel.shape[0]
    rows_local = left_panel.shape[1]
    cols_local = right_panel.shape[1]
    channels = incoming_adjoint_couple.shape[2]
    step_rows = math.gcd(rows_local, 16)
    count = rows_local // step_rows
    left_blocks = left_panel.reshape(seq_total, count, step_rows, width).transpose(1, 0, 2, 3)
    cot_blocks = incoming_adjoint_couple.reshape(count, step_rows, cols_local, channels)
    bias_wide = couple_offset_vector.astype(jnp.float32)
    weight_back = couple_mapping_matrix.T

    def advance(carry, inputs):
        weight_sum, right_sum = carry
        left_block, cot_block = inputs
        outer = (
            jnp.einsum("sic,sje->ijce", left_block, right_panel, preferred_element_type=jnp.float32)
            / seq_total
        )
        flat = outer.astype(jnp.bfloat16).reshape(step_rows * cols_local, width * width)
        update = (
            jnp.dot(flat, couple_mapping_matrix, preferred_element_type=jnp.float32) + bias_wide
        ).astype(jnp.bfloat16)
        grad_rows = cot_block.reshape(step_rows * cols_local, channels)
        outer_grad = jnp.dot(grad_rows, weight_back, preferred_element_type=jnp.float32).astype(
            jnp.bfloat16
        )
        outer_grad = outer_grad.reshape(step_rows, cols_local, width, width)
        weight_sum = weight_sum + lax.dot_general(
            flat, grad_rows, (((0,), (0,)), ((), ())), preferred_element_type=jnp.float32
        )
        left_grad = (
            jnp.einsum("ijce,sje->sic", outer_grad, right_panel, preferred_element_type=jnp.float32)
            / seq_total
        )
        right_sum = (
            right_sum
            + jnp.einsum(
                "ijce,sic->sje", outer_grad, left_block, preferred_element_type=jnp.float32
            )
            / seq_total
        )
        return (
            (weight_sum, right_sum),
            (update.reshape(step_rows, cols_local, channels), left_grad),
        )

    start = (
        jnp.zeros((width * width, channels), jnp.float32),
        jnp.zeros((seq_total, cols_local, width), jnp.float32),
    )
    (weight_part, right_grad), (updates, left_grads) = lax.scan(
        advance, start, (left_blocks, cot_blocks)
    )
    pair_delta_output = updates.reshape(rows_local, cols_local, channels)
    left_grad = left_grads.transpose(1, 0, 2, 3).reshape(seq_total, rows_local, width)
    left_summed = summed_on_arrival(
        regroup(left_grad, rows_count, cols_count).astype(jnp.bfloat16), "col", 0
    ).astype(jnp.bfloat16)
    left_back = lax.all_to_all(left_summed, "row", split_axis=0, concat_axis=1, tiled=True)
    right_summed = summed_on_arrival(right_grad.astype(jnp.bfloat16), "row", 0).astype(jnp.bfloat16)
    right_back = lax.all_to_all(right_summed, "col", split_axis=0, concat_axis=1, tiled=True)
    factor_weight_gradient = lax.psum(weight_part, ("row", "col"))
    both = jnp.concatenate([left_back, right_back], axis=-1)
    normalized_gradient = jnp.dot(both, split_mapping_matrix.T, preferred_element_type=jnp.float32)
    first_factor = jnp.mean(normalized_gradient, axis=-1, keepdims=True)
    second_factor = jnp.mean(normalized_gradient * standardized_activations, axis=-1, keepdims=True)
    alignment_gradient = (
        reciprocal_spread
        * (normalized_gradient - first_factor - standardized_activations * second_factor)
    ).astype(jnp.bfloat16)
    return (pair_delta_output, alignment_gradient, factor_weight_gradient)


def solution(mesh):
    placed = (P(("row", "col"), None, None), P(), P(), P(), P("row", "col", None))
    return jax.shard_map(
        on_device,
        mesh=mesh,
        in_specs=placed,
        out_specs=(P("row", "col", None), P(("row", "col"), None, None), P()),
        check_vma=False,
    )
```

profile of v0, /device:TPU:1, one launch (start us, length us, event | category | flops | bytes accessed | tf_op | source)
XLA Modules:
  0.0 425.5 jit_solution(13450894267339800620)
XLA Ops:
  14.4 9.3 %all-to-all-start = ((bf16[16,2,1024]{2,1,0:T(2,128)(2,1)}), bf16[16,2,1024]{2,1,0:T(2,128)(2,1)S(1)}, u32[]{:S(2)}, u32[]{:S(2)}) async-start(bf16[16,2,1024]{2,1,0:T(2,128)(2,1)} %reshape.113), calls=%async_computation | async-start | bytes 131072 | tf_op jit(solution)/shard_map/all_to_all | solution.py:68
  27.2 3.8 all-to-all-done
  31.0 4.5 %all-to-all-start.2 = ((bf16[8,2,2048]{2,1,0:T(2,128)(2,1)}), bf16[8,2,2048]{2,1,0:T(2,128)(2,1)S(1)}, u32[]{:S(2)}, u32[]{:S(2)}) async-start(bf16[8,2,2048]{2,1,0:T(2,128)(2,1)} %reshape.117), calls=%async_computation.2 | async-start | bytes 131072 | tf_op jit(solution)/shard_map/all_to_all | solution.py:70
  44.8 7.0 %all-to-all-done.1 = bf16[8,2,16384]{2,1,0:T(2,128)(2,1)S(1)} async-done(((bf16[8,2,16384]{2,1,0:T(2,128)(2,1)}), bf16[8,2,16384]{2,1,0:T(2,128)(2,1)S(1)}, u32[]{:S(2)}, u32[]{:S(2)}) %all-to-all-start.1) | async-done | bytes 524320 | tf_op jit(solution)/shard_map/all_to_all | solution.py:11
  53.0 6.9 %all-to-all-start.3 = ((bf16[16,8,128,32]{2,1,3,0:T(8,128)(2,1)}), bf16[16,8,128,32]{2,1,3,0:T(8,128)(2,1)}, u32[]{:S(2)}, u32[]{:S(2)}) async-start(bf16[16,8,128,32]{2,1,3,0:T(8,128)(2,1)} %broadcast_in_dim.48), calls=%async_computation.3 | async-start | bytes 2097152 | tf_op jit(solution)/shard_map/all_to_all | solution.py:11
  64.9 3.9 copy.45
  68.8 8.3 %all-to-all-done.3 = bf16[16,8,128,32]{2,1,3,0:T(8,128)(2,1)} async-done(((bf16[16,8,128,32]{2,1,3,0:T(8,128)(2,1)}), bf16[16,8,128,32]{2,1,3,0:T(8,128)(2,1)}, u32[]{:S(2)}, u32[]{:S(2)}) %all-to-all-start.3) | async-done | bytes 1048608 | tf_op jit(solution)/shard_map/all_to_all | solution.py:11
  78.9 128.3 %while.17 = (s32[]{:T(128)}, f32[1024,128]{1,0:T(8,128)}, f32[128,128,32]{1,0,2:T(8,128)S(1)}, bf16[4,16,128,128]{3,2,1,0:T(8,128)(2,1)}, bf16[4,128,16,32]{1,2,...) while((s32[]{:T(128)}, f32[1024,128]{1,0:T(8,128)}, ...), condition=%wide.region_3.4_spmd.clone, body=%wide.region_2.3_spmd.clone.sunk | while | flops 3229941760 | bytes 96995688 | solution.py:122
  88.1 3.5 fusion.90
  94.8 6.5 %copy.92 = bf16[2048,1024]{0,1:T(8,128)(2,1)} copy(bf16[2048,1024]{1,0:T(8,128)(2,1)} %convolution_convert_fusion.3) | data formatting | bytes 8388608 | tf_op jit(solution)/shard_map/while/body/eval_jaxpr/convert_element_type | solution.py:95
  101.3 3.6 copy.93
  104.9 4.1 fusion.91
  120.1 3.5 fusion.90
  126.8 6.5 %copy.92 = bf16[2048,1024]{0,1:T(8,128)(2,1)} copy(bf16[2048,1024]{1,0:T(8,128)(2,1)} %convolution_convert_fusion.3) | data formatting | bytes 8388608 | tf_op jit(solution)/shard_map/while/body/eval_jaxpr/convert_element_type | solution.py:95
  133.3 3.6 copy.93
  136.9 4.1 fusion.91
  152.1 3.5 fusion.90
  158.8 6.5 %copy.92 = bf16[2048,1024]{0,1:T(8,128)(2,1)} copy(bf16[2048,1024]{1,0:T(8,128)(2,1)} %convolution_convert_fusion.3) | data formatting | bytes 8388608 | tf_op jit(solution)/shard_map/while/body/eval_jaxpr/convert_element_type | solution.py:95
  165.4 3.6 copy.93
  169.0 4.1 fusion.91
  184.1 3.5 fusion.90
  190.8 6.5 %copy.92 = bf16[2048,1024]{0,1:T(8,128)(2,1)} copy(bf16[2048,1024]{1,0:T(8,128)(2,1)} %convolution_convert_fusion.3) | data formatting | bytes 8388608 | tf_op jit(solution)/shard_map/while/body/eval_jaxpr/convert_element_type | solution.py:95
  197.4 3.6 copy.93
  201.0 4.1 fusion.91
  207.2 5.3 %copy.47 = bf16[128,4,16,32]{3,2,1,0:T(8,128)(2,1)} copy(bf16[128,4,16,32]{0,2,3,1:T(8,128)(2,1)} %bitcast.181) | data formatting | bytes 1048576 | tf_op jit(solution)/shard_map/convert_element_type | solution.py:128
  222.2 6.0 %all-to-all-done.4 = bf16[8,2,16384]{2,1,0:T(2,128)(2,1)S(1)} async-done(((bf16[8,2,16384]{2,1,0:T(2,128)(2,1)}), bf16[8,2,16384]{2,1,0:T(2,128)(2,1)S(1)}, u32[]{:S(2)}, u32[]{:S(2)}) %all-to-all-start.4) | async-done | bytes 524320 | tf_op jit(solution)/shard_map/all_to_all | solution.py:34
  228.2 5.7 %all-to-all-start.6 = ((bf16[16,8,128,32]{2,1,3,0:T(8,128)(2,1)}), bf16[16,8,128,32]{2,1,3,0:T(8,128)(2,1)S(1)}, u32[]{:S(2)}, u32[]{:S(2)}) async-start(bf16[16,8,128,32]{2,1,3,0:T(8,128)(2,1)} %copy.51), calls=%async_computation.6 | async-start | bytes 2097152 | tf_op jit(solution)/shard_map/all_to_all | solution.py:34
  235.6 15.3 %all-to-all-done.6 = bf16[16,8,128,32]{2,1,3,0:T(8,128)(2,1)S(1)} async-done(((bf16[16,8,128,32]{2,1,3,0:T(8,128)(2,1)}), bf16[16,8,128,32]{2,1,3,0:T(8,128)(2,1)S(1)}, u32[]{:S(2)}, u32[]{:S(2)}) %all-to-all-start.6) | async-done | bytes 1048608 | tf_op jit(solution)/shard_map/all_to_all | solution.py:34
  250.9 4.4 %all-to-all-start.5 = ((bf16[16,2,1024]{2,1,0:T(2,128)(2,1)}), bf16[16,2,1024]{2,1,0:T(2,128)(2,1)S(1)}, u32[]{:S(2)}, u32[]{:S(2)}) async-start(bf16[16,2,1024]{2,1,0:T(2,128)(2,1)} %reshape.121), calls=%async_computation.5 | async-start | bytes 131072 | tf_op jit(solution)/shard_map/all_to_all | solution.py:130
  256.0 6.6 %all-to-all-done.5 = bf16[16,2,1024]{2,1,0:T(2,128)(2,1)S(1)} async-done(((bf16[16,2,1024]{2,1,0:T(2,128)(2,1)}), bf16[16,2,1024]{2,1,0:T(2,128)(2,1)S(1)}, u32[]{:S(2)}, u32[]{:S(2)}) %all-to-all-start.5) | async-done | bytes 65568 | tf_op jit(solution)/shard_map/all_to_all | solution.py:130
  267.1 3.9 all-to-all-done.7
  272.1 144.7 %all-reduce.2.cloned.1.call-done = f32[1024,128]{1,0:T(8,128)} async-done(((f32[1024,128]{1,0:T(8,128)}), f32[1024,128]{1,0:T(8,128)}) %all-reduce.2.cloned.1.call-update) | async-done | bytes 524304 | tf_op jit(solution)/shard_map/psum | solution.py:133
  (155 shorter events, 104.1 us)
Async XLA Ops:
  14.4 16.7 %all-to-all-start = ((bf16[16,2,1024]{2,1,0:T(2,128)(2,1)}), bf16[16,2,1024]{2,1,0:T(2,128)(2,1)S(1)}, u32[]{:S(2)}, u32[]{:S(2)}) async-start(bf16[16,2,1024]{2,1,0:T(2,128)(2,1)} %reshape.113), calls=%async_computation | async-start | bytes 131072 | tf_op jit(solution)/shard_map/all_to_all | solution.py:68
  31.0 9.6 %all-to-all-start.2 = ((bf16[8,2,2048]{2,1,0:T(2,128)(2,1)}), bf16[8,2,2048]{2,1,0:T(2,128)(2,1)S(1)}, u32[]{:S(2)}, u32[]{:S(2)}) async-start(bf16[8,2,2048]{2,1,0:T(2,128)(2,1)} %reshape.117), calls=%async_computation.2 | async-start | bytes 131072 | tf_op jit(solution)/shard_map/all_to_all | solution.py:70
  36.3 23.5 %copy-start.9 = (bf16[1024,128]{1,0:T(8,128)(2,1)S(1)}, bf16[1024,128]{1,0:T(8,128)(2,1)}, u32[]{:S(2)}) copy-start(bf16[1024,128]{1,0:T(8,128)(2,1)} %param.9) | copy-start | bytes 786436
  36.3 23.7 %copy-start.11 = (bf16[128]{0:T(256)(128)(2,1)S(1)}, bf16[128]{0:T(256)(128)(2,1)}, u32[]{:S(2)}) copy-start(bf16[128]{0:T(256)(128)(2,1)} %param.10) | copy-start | bytes 772
  40.6 11.2 %all-to-all-start.1 = ((bf16[8,2,16384]{2,1,0:T(2,128)(2,1)}), bf16[8,2,16384]{2,1,0:T(2,128)(2,1)S(1)}, u32[]{:S(2)}, u32[]{:S(2)}) async-start(bf16[8,2,16384]{2,1,0:T(2,128)(2,1)} %reshape.115), calls=%async_computation.1 | async-start | bytes 1048576 | tf_op jit(solution)/shard_map/all_to_all | solution.py:11
  53.0 24.0 %all-to-all-start.3 = ((bf16[16,8,128,32]{2,1,3,0:T(8,128)(2,1)}), bf16[16,8,128,32]{2,1,3,0:T(8,128)(2,1)}, u32[]{:S(2)}, u32[]{:S(2)}) async-start(bf16[16,8,128,32]{2,1,3,0:T(8,128)(2,1)} %broadcast_in_dim.48), calls=%async_computation.3 | async-start | bytes 2097152 | tf_op jit(solution)/shard_map/all_to_all | solution.py:11
  79.1 5.1 %copy-start.2 = (bf16[128,128,32]{1,0,2:T(8,128)(2,1)}, bf16[128,128,32]{1,0,2:T(8,128)(2,1)S(1)}, u32[]{:S(2)}) copy-start(bf16[128,128,32]{1,0,2:T(8,128)(2,1)S(1)} %get-tuple-element.269) | copy-start | bytes 3145732 | tf_op jit(solution)/shard_map/while
  84.1 4.0 copy-start.1
  84.2 3.9 copy-start.7
  104.9 4.1 copy-start.3
  104.9 4.1 copy-start.5
  111.2 5.0 %copy-start.2 = (bf16[128,128,32]{1,0,2:T(8,128)(2,1)}, bf16[128,128,32]{1,0,2:T(8,128)(2,1)S(1)}, u32[]{:S(2)}) copy-start(bf16[128,128,32]{1,0,2:T(8,128)(2,1)S(1)} %get-tuple-element.269) | copy-start | bytes 3145732 | tf_op jit(solution)/shard_map/while
  116.2 4.0 copy-start.1
  116.2 3.9 copy-start.7
  136.9 4.1 copy-start.3
  136.9 4.1 copy-start.5
  143.2 5.0 %copy-start.2 = (bf16[128,128,32]{1,0,2:T(8,128)(2,1)}, bf16[128,128,32]{1,0,2:T(8,128)(2,1)S(1)}, u32[]{:S(2)}) copy-start(bf16[128,128,32]{1,0,2:T(8,128)(2,1)S(1)} %get-tuple-element.269) | copy-start | bytes 3145732 | tf_op jit(solution)/shard_map/while
  148.2 4.0 copy-start.1
  148.2 3.9 copy-start.7
  168.9 4.1 copy-start.3
  169.0 4.1 copy-start.5
  175.2 5.0 %copy-start.2 = (bf16[128,128,32]{1,0,2:T(8,128)(2,1)}, bf16[128,128,32]{1,0,2:T(8,128)(2,1)S(1)}, u32[]{:S(2)}) copy-start(bf16[128,128,32]{1,0,2:T(8,128)(2,1)S(1)} %get-tuple-element.269) | copy-start | bytes 3145732 | tf_op jit(solution)/shard_map/while
  180.2 4.0 copy-start.1
  180.2 3.9 copy-start.7
  201.0 4.1 copy-start.3
  201.0 4.1 copy-start.5
  216.1 12.1 %all-to-all-start.4 = ((bf16[8,2,16384]{2,1,0:T(2,128)(2,1)}), bf16[8,2,16384]{2,1,0:T(2,128)(2,1)S(1)}, u32[]{:S(2)}, u32[]{:S(2)}) async-start(bf16[8,2,16384]{2,1,0:T(2,128)(2,1)} %reshape.119), calls=%async_computation.4 | async-start | bytes 1048576 | tf_op jit(solution)/shard_map/all_to_all | solution.py:34
  222.2 48.9 %copy-start.4 = (bf16[1,1024,64]{1,2,0:T(8,128)(2,1)S(1)}, bf16[1,1024,64]{1,2,0:T(8,128)(2,1)}, u32[]{:S(2)}) copy-start(bf16[1,1024,64]{1,2,0:T(8,128)(2,1)} %param.7) | copy-start | bytes 393220
  228.2 22.7 %all-to-all-start.6 = ((bf16[16,8,128,32]{2,1,3,0:T(8,128)(2,1)}), bf16[16,8,128,32]{2,1,3,0:T(8,128)(2,1)S(1)}, u32[]{:S(2)}, u32[]{:S(2)}) async-start(bf16[16,8,128,32]{2,1,3,0:T(8,128)(2,1)} %copy.51), calls=%async_computation.6 | async-start | bytes 2097152 | tf_op jit(solution)/shard_map/all_to_all | solution.py:34
  250.9 11.8 %all-to-all-start.5 = ((bf16[16,2,1024]{2,1,0:T(2,128)(2,1)}), bf16[16,2,1024]{2,1,0:T(2,128)(2,1)S(1)}, u32[]{:S(2)}, u32[]{:S(2)}) async-start(bf16[16,2,1024]{2,1,0:T(2,128)(2,1)} %reshape.121), calls=%async_computation.5 | async-start | bytes 131072 | tf_op jit(solution)/shard_map/all_to_all | solution.py:130
  262.7 8.4 %all-to-all-start.7 = ((bf16[8,128,32]{1,2,0:T(8,128)(2,1)}), bf16[8,128,32]{1,2,0:T(8,128)(2,1)S(1)}, u32[]{:S(2)}, u32[]{:S(2)}) async-start(bf16[8,128,32]{1,2,0:T(8,128)(2,1)} %copy.53), calls=%async_computation.7 | async-start | bytes 131072 | tf_op jit(solution)/shard_map/all_to_all | solution.py:132
  266.0 150.8 %all-reduce.2.cloned.1.call-start = ((), (), s32[]{:S(2)}) async-start(), calls=%async_computation.8 | async-start | bytes 1048576 | tf_op jit(solution)/shard_map/psum | solution.py:133
  (13 other events, 28.9 us)
Sparse Core Ops, SparseCore 0:
  272.2 144.5 all-reduce.1
where the time goes:
time: 428 us; the launch traced here: 426 us
  waiting for transfers between devices  199 us (46%)
  local copies, waits for them, and re-layouts  96.1 us (22%)
  matrix products  66.7 us (16%)
  starting transfers between devices  41.1 us (10%)
  between operations  14.4 us (3%)
  other arithmetic  7.57 us (2%)
    psum x1, waiting for transfers between devices, on_device(): factor_weight_gradient = lax.psum(weight_part, ('row', 'col'))  145 us
    convert_element_type x4, local copies, waits for them, and re-layouts, advance(): jnp.dot(grad_rows, weight_back, preferred_element_type=jnp.float32)  26.1 us
    all_to_all x2, waiting for transfers between devices, summed_on_arrival(): pieces = lax.all_to_all(cut_along(array, dim, size), axis, 0, 0, tiled=True)  21.3 us
    while x68, local copies, waits for them, and re-layouts  17.6 us
    dot_general x4, matrix products, advance(): jnp.einsum('ijce,sic->sje', outer_grad, left_block, preferred_element_typ...  16.3 us
    unnamed x25, local copies, waits for them, and re-layouts  15.8 us
    all_to_all x2, waiting for transfers between devices, copy_for_each(): lax.all_to_all(jnp.broadcast_to(array[None], (size, *array.shape)), axis,...  15.2 us
    dot_general x4, matrix products, advance(): lax.dot_general(flat, grad_rows, (((0,), (0,)), ((), ())), preferred_elem...  14 us
  transfers between devices with their start and end apart: 9, of which 9 were waited for; matrix products, arithmetic and copies ran while one was open for 5% of the time, Pallas kernels for 0%

commit v1 on v0

v1 whole, which is shorter than its diff:
```python
import functools

import jax
import jax.numpy as jnp
from jax import lax
from jax.experimental import pallas as pl
from jax.experimental.pallas import tpu as pltpu
from jax.sharding import PartitionSpec as P

BF = jnp.bfloat16
F32 = jnp.float32
MESH = pl.DeviceIdType.MESH
NT = (((1,), (1,)), ((), ()))
DMA = pltpu.SemaphoreType.DMA


def dot(a, b):
    return jnp.dot(a, b, preferred_element_type=F32)


def dnt(a, b):
    return lax.dot_general(a, b, NT, preferred_element_type=F32)


def place():
    r, q = lax.axis_index("row"), lax.axis_index("col")
    y, zh, c = lax.div(r, 4), lax.rem(lax.div(r, 2), 2), lax.rem(r, 2)
    x, zl = lax.div(q, 2), lax.rem(q, 2)
    return r, q, y, zh, c, x, zl


def row_of(y, zh, c):
    return y * 4 + zh * 2 + c


def remote(src, dst, send, recv, to):
    return pltpu.make_async_remote_copy(
        src_ref=src, dst_ref=dst, send_sem=send, recv_sem=recv, device_id=to, device_id_type=MESH
    )


def greet(r, q):
    barrier = pltpu.get_barrier_semaphore()
    for d in range(1, 16):
        pl.semaphore_signal(barrier, inc=1, device_id=(lax.rem(r + d, 16), q), device_id_type=MESH)
    for d in range(1, 8):
        pl.semaphore_signal(barrier, inc=1, device_id=(r, lax.rem(q + d, 8)), device_id_type=MESH)


def greeted():
    pl.semaphore_wait(pltpu.get_barrier_semaphore(), 22)


def standardized(x_ref):
    x = x_ref[0].astype(F32)
    centred = x - jnp.mean(x, axis=-1, keepdims=True)
    rstd = lax.rsqrt(jnp.mean(centred * centred, axis=-1, keepdims=True) + 1e-5)
    return centred * rstd, rstd


def widened(ws, t):
    left = ws[:, :32]
    tiled = jnp.concatenate([left] * 4, axis=1)
    lane = lax.broadcasted_iota(jnp.int32, (64, 128), 1)
    return jnp.where(lane // 32 == t, tiled, 0.0).astype(BF)


def swapped(outer, inner):
    n = outer * inner
    to = lax.broadcasted_iota(jnp.int32, (n, n), 0)
    at = lax.broadcasted_iota(jnp.int32, (n, n), 1)
    return (at == (to % outer) * inner + to // outer).astype(F32).astype(BF)


def project(ws, xhat, xs, lsend, rsend):
    xs[...] = xhat
    for t in range(4):
        part = xs[pl.ds(t, 256, stride=4), :].astype(BF)
        term = dot(part, widened(ws, t))
        acc = term if t == 0 else acc + term
    lsend[...] = acc.astype(BF).reshape(16, 16, 128)
    right = ws.T[32:, :].astype(BF)
    for q in range(8):
        rsend[q] = dnt(right, xs[q * 128 : (q + 1) * 128, :].astype(BF)).astype(BF)


def scatter_start(r, q, lsend, rsend, l1, r1, sems):
    ls, lr, rs, rr = sems
    out = []
    for d in range(1, 16):
        to = lax.rem(r + d, 16)
        cp = remote(lsend.at[to], l1.at[r], ls.at[d], lr.at[r], (to, q))
        cp.start()
        out.append(cp)
    for d in range(1, 8):
        to = lax.rem(q + d, 8)
        cp = remote(rsend.at[to], r1.at[q], rs.at[d], rr.at[q], (r, to))
        cp.start()
        out.append(cp)
    return out


def wait_row(r, q, buf, recv, send):
    for d in range(1, 16):
        at = lax.rem(r + d, 16)
        remote(buf.at[at], buf.at[at], send.at[d], recv.at[at], (at, q)).wait_recv()


def wait_col(r, q, buf, recv, send):
    for d in range(1, 8):
        at = lax.rem(q + d, 8)
        remote(buf.at[at], buf.at[at], send.at[d], recv.at[at], (r, at)).wait_recv()


class Sends:
    def __init__(self, buf, send, recv):
        self.buf, self.send, self.recv, self.n, self.all = buf, send, recv, 0, []

    def start(self, slot, to):
        ref = self.buf.at[:, slot]
        cp = remote(ref, ref, self.send.at[self.n], self.recv.at[slot], to)
        self.n += 1
        cp.start()
        self.all.append(cp)

    def arrived(self, slot, source):
        ref = self.buf.at[:, slot]
        remote(ref, ref, self.send.at[0], self.recv.at[slot], source).wait_recv()


def spread_left(p, sends):
    r, q, y, zh, c, x, zl = p
    over = x * 2 + 1 - zl
    sends.start(q, (r, over))
    for d in (1, 3, 2):
        sends.start(q, (r, lax.rem(x + d, 4) * 2 + zl))

    def relay():
        sends.arrived(over, (r, over))
        for d in (1, 3, 2):
            sends.start(over, (r, lax.rem(x + d, 4) * 2 + zl))

    def rest():
        for d in (1, 3, 2):
            xd = lax.rem(x + d, 4)
            sends.arrived(xd * 2 + zl, (r, xd * 2 + zl))
            sends.arrived(xd * 2 + 1 - zl, (r, xd * 2 + zl))

    return relay, rest


def spread_right(p, sends):
    r, q, y, zh, c, x, zl = p
    over = row_of(y, 1 - zh, c)
    mate = row_of(y, zh, 1 - c)
    sends.start(r, (over, q))
    for d in (1, 3, 2):
        sends.start(r, (row_of(lax.rem(y + d, 4), zh, c), q))
    sends.start(r, (mate, q))

    def relay():
        sends.arrived(over, (over, q))
        for d in (1, 3, 2):
            sends.start(over, (row_of(lax.rem(y + d, 4), zh, c), q))
        sends.start(over, (mate, q))

    def rest():
        for zz in (zh, 1 - zh):
            for d in (1, 3, 2):
                yd = lax.rem(y + d, 4)
                slot = row_of(yd, zz, c)
                sends.arrived(slot, (row_of(yd, zh, c), q))
                sends.start(slot, (mate, q))
        for zz in (zh, 1 - zh):
            for d in range(4):
                sends.arrived(row_of(lax.rem(y + d, 4), zz, 1 - c), (mate, q))

    return relay, rest


def natural_left(l3, l4, lt):
    order = swapped(8, 16)
    for a in range(16):
        rows = dot(order, l3[a].reshape(128, 128)) * (1.0 / 128.0)
        l4[a] = rows.astype(BF)
        lt[a * 128 : (a + 1) * 128, :] = rows.T.astype(BF)


def forward_kernel(x, ws_ref, l4, lt, rn, xs, lsend, rsend, l1, r1, l3, r3, ls, lr, rs, rr, l2s, l2r, r2s, r2r):
    p = place()
    r, q = p[0], p[1]
    greet(r, q)
    ws = ws_ref[...].astype(F32)
    xhat, _ = standardized(x)
    project(ws, xhat, xs, lsend, rsend)
    l1[r] = lsend[r]
    r1[q] = rsend[q]
    greeted()
    out = scatter_start(r, q, lsend, rsend, l1, r1, (ls, lr, rs, rr))
    left_order, right_order = swapped(16, 16), swapped(8, 32)
    wait_col(r, q, r1, rr, rs)
    r3[:, r] = dot(right_order, r1[...].reshape(256, 128)).reshape(32, 8, 128).astype(BF)
    rsends = Sends(r3, r2s, r2r)
    rrelay, rrest = spread_right(p, rsends)
    wait_row(r, q, l1, lr, ls)
    l3[:, q] = dot(left_order, l1[...].reshape(256, 128)).astype(BF).reshape(16, 16, 128)
    lsends = Sends(l3, l2s, l2r)
    lrelay, lrest = spread_left(p, lsends)
    rrelay()
    lrelay()
    lrest()
    natural_left(l3, l4, lt)
    rrest()
    for e in range(32):
        rn[e] = r3[e].reshape(128, 128)
    for cp in out + rsends.all + lsends.all:
        cp.wait_send()


def grad_outer(cot, wr, G, unroll):
    @pl.loop(0, 32 // unroll)
    def _(step):
        for u in range(unroll):
            p = step * unroll + u
            o = dnt(wr[...], cot[pl.ds(2 * p, 2)].reshape(256, 128)).astype(BF)
            for h in range(2):
                G[:, pl.ds(pl.multiple_of((2 * p + h) * 32, 32), 32), :] = o[:, h * 128 : (h + 1) * 128].reshape(32, 32, 128)


def outer_product(lt, R, O, unroll):
    @pl.loop(0, 16 // unroll)
    def _(step):
        for u in range(unroll):
            p = step * unroll + u
            o = dot(lt[...], jnp.concatenate([R[2 * p], R[2 * p + 1]], axis=1)).astype(BF)
            O[2 * p] = o[:, :128]
            O[2 * p + 1] = o[:, 128:]


def left_gradient(G, R, put, M):
    @pl.loop(0, 2048 // M)
    def _(m):
        rows = pl.ds(pl.multiple_of(m * M, M), M)
        for p in range(16):
            g = jnp.concatenate([G[2 * p, rows, :], G[2 * p + 1, rows, :]], axis=1)
            term = dnt(g, jnp.concatenate([R[2 * p], R[2 * p + 1]], axis=1))
            acc = term if p == 0 else acc + term
        put(m, acc * (1.0 / 128.0))


def right_gradient(G, l4, put, unroll):
    @pl.loop(0, 16 // unroll)
    def _(step):
        for u in range(unroll):
            p = step * unroll + u
            for k in range(8):
                rows = slice(k * 256, (k + 1) * 256)
                g = jnp.concatenate([G[2 * p, rows, :], G[2 * p + 1, rows, :]], axis=1)
                term = dot(jnp.concatenate([l4[2 * k], l4[2 * k + 1]], axis=1), g)
                acc = term if k == 0 else acc + term
            put(2 * p, acc[:, :128])
            put(2 * p + 1, acc[:, 128:])


def weight_gradient(O, cot, put, E):
    @pl.loop(0, 32 // E)
    def _(m):
        for p in range(32):
            x = jnp.concatenate(
                [O[pl.ds(m * E, E), (2 * p + h) * 32 : (2 * p + h + 1) * 32, :].reshape(E * 32, 128) for h in range(2)], axis=1
            )
            term = dot(x, cot[2 * p : 2 * p + 2].reshape(256, 128))
            acc = term if p == 0 else acc + term
        put(m, acc)


def of_row(O, i):
    return O[:, pl.ds(pl.multiple_of(i * 32, 32), 32), :].reshape(1024, 128)


def pair_update(O, wt, bias, out, unroll):
    @pl.loop(0, 32 // unroll)
    def _(step):
        for u in range(unroll):
            p = step * unroll + u
            y = dot(wt[...], jnp.concatenate([of_row(O, 2 * p), of_row(O, 2 * p + 1)], axis=1))
            for h in range(2):
                out[2 * p + h] = (y[:, h * 128 : (h + 1) * 128].T + bias[...]).astype(BF)


def middle_kernel(l4, lt, rn, cot, wr, wt, bias, out, lg, rg, wg, O, G):
    order = swapped(16, 8)
    grad_outer(cot, wr, G, 8)

    def put_right(e, v):
        rg[e] = v.reshape(8, 2, 8, 128).astype(BF)

    right_gradient(G, l4, put_right, 8)

    def put_left(m, v):
        v = v.astype(BF)
        for k in range(4):
            lg[m * 4 + k] = dnt(order, v[k * 128 : (k + 1) * 128, :]).astype(BF)

    left_gradient(G, rn, put_left, 512)
    outer_product(lt, rn, O, 4)

    def put_weight(m, v):
        wg[pl.ds(m * 4, 4)] = v.astype(BF).reshape(4, 64, 128)

    weight_gradient(O, cot, put_weight, 8)
    pair_update(O, wt, bias, out, 8)


def to_row(p, src, dst, send, recv):
    r, q = p[0], p[1]
    out = []
    for d in range(1, 16):
        to = lax.rem(r + d, 16)
        cp = remote(src(to), dst.at[r], send.at[d], recv.at[r], (to, q))
        cp.start()
        out.append(cp)
    return out


def to_col(p, src, dst, send, recv):
    r, q = p[0], p[1]
    out = []
    for d in range(1, 8):
        to = lax.rem(q + d, 8)
        cp = remote(src(to), dst.at[q], send.at[d], recv.at[q], (r, to))
        cp.start()
        out.append(cp)
    return out


def summed(buf, n):
    acc = buf[0].astype(F32)
    for k in range(1, n):
        acc = acc + buf[k].astype(F32)
    return acc


def backward_kernel(
    x, ws_ref, lg, rg, wg, grad, wout,
    ns, rc, rcs, ry, rys, rz, r6, rin, lx, lxs, lz, l6, lin, wr_, ws_sum, wc, wall, wf,
    one_s, one_r, ys, yr, xs_, xr, lo_s, lo_r, ro_s, ro_r, w1s, w1r, w2s, w2r, w3s, w3r,
):
    p = place()
    r, q, y, zh, c, xx, zl = p
    greet(r, q)
    ws = ws_ref[...].astype(F32)
    xhat, rstd = standardized(x)
    greeted()
    sent = []
    mate = (row_of(y, zh, 1 - c), q)
    core = remote(rg.at[:, :, 1 - c], rc, one_s.at[0], one_r.at[0], mate)
    core.start()
    xcp = []
    for d in (1, 3, 2):
        to = lax.rem(xx + d, 4)
        cp = remote(lg.at[:, pl.ds(to * 32, 32), :], lx.at[d - 1], xs_.at[d - 1], xr.at[d - 1], (r, to * 2 + zl))
        cp.start()
        xcp.append(cp)
    sent += to_row(p, lambda to: wg.at[to], wr_, w1s, w1r)
    wr_[r] = wg[r]
    core.wait_recv()
    for e in range(32):
        rcs[e] = (rg[e, :, c].astype(F32) + rc[e].astype(F32)).astype(BF)
    ycp = []
    for d in (1, 3, 2):
        to = lax.rem(y + d, 4)
        cp = remote(rcs.at[:, pl.ds(to * 2, 2)], ry.at[d - 1], ys.at[d - 1], yr.at[d - 1], (row_of(to, zh, c), q))
        cp.start()
        ycp.append(cp)
    wait_row(r, q, wr_, w1r, w1s)
    ws_sum[...] = summed(wr_, 16).astype(BF)
    wc[q] = ws_sum[...]
    sent += to_col(p, lambda to: ws_sum, wc, w2s, w2r)
    for cp in xcp:
        cp.wait_recv()
    for a in range(16):
        own = lg[a, pl.ds(pl.multiple_of(xx * 32, 32), 32), :].astype(F32)
        for d in range(3):
            own = own + lx[d, a].astype(F32)
        lxs[a] = own.astype(BF).reshape(2, 16, 128)
    lzc = remote(lxs.at[:, 1 - zl], lz, one_s.at[1], one_r.at[1], (r, xx * 2 + 1 - zl))
    lzc.start()
    wait_col(r, q, wc, w2r, w2s)
    wall[r] = summed(wc, 8).astype(BF)
    sent += to_row(p, lambda to: wall.at[r], wall, w3s, w3r)
    lzc.wait_recv()
    five = (lxs[:, zl].astype(F32) + lz[...].astype(F32)).astype(BF)
    l6[...] = dot(swapped(16, 16), five.reshape(256, 128)).astype(BF).reshape(16, 16, 128)
    lin[r] = l6[r]
    sent += to_row(p, lambda to: l6.at[to], lin, lo_s, lo_r)
    for cp in ycp:
        cp.wait_recv()
    for e in range(32):
        own = rcs[e, pl.ds(y * 2, 2)].astype(F32)
        for d in range(3):
            own = own + ry[d, e].astype(F32)
        rys[e] = own.astype(BF)
    rzc = remote(rys.at[:, 1 - zh], rz, one_s.at[2], one_r.at[2], (row_of(y, 1 - zh, c), q))
    rzc.start()
    rzc.wait_recv()
    five = rys[:, zh].astype(F32) + rz[...].astype(F32)
    r6[...] = dot(swapped(32, 8), five.reshape(256, 128).astype(BF)).astype(BF).reshape(8, 32, 128)
    rin[q] = r6[q]
    sent += to_col(p, lambda to: r6.at[to], rin, ro_s, ro_r)
    wait_row(r, q, lin, lo_r, lo_s)
    flat = lin[...].reshape(256, 128)
    for t in range(4):
        ns[pl.ds(t, 256, stride=4), :] = dnt(flat, widened(ws, t))
    wait_row(r, q, wall, w3r, w3s)
    for k in range(16):
        wf[k * 64 : (k + 1) * 64, :] = wall[k].astype(F32)
    for k in range(32):
        wout[k * 32 : (k + 1) * 32, :] = wf[pl.ds(k, 32, stride=32), :]
    wait_col(r, q, rin, ro_r, ro_s)
    right = ws[:, 32:].astype(BF)
    for k in range(8):
        rows = slice(k * 128, (k + 1) * 128)
        ns[rows, :] = ns[rows, :] + dnt(rin[k].astype(F32).T.astype(BF), right)
    ng = ns[...]
    first = jnp.mean(ng, axis=-1, keepdims=True)
    second = jnp.mean(ng * xhat, axis=-1, keepdims=True)
    grad[0] = (rstd * (ng - first - xhat * second)).astype(BF)
    for cp in [core, lzc, rzc] + xcp + ycp + sent:
        cp.wait_send()


VM = pl.BlockSpec(memory_space=pltpu.VMEM)


def call(kernel, outs, n_in, scratch, name, ident=None):
    extra = {} if ident is None else {"collective_id": ident, "has_side_effects": True}
    return pl.pallas_call(
        kernel,
        out_shape=tuple(jax.ShapeDtypeStruct(s, t) for s, t in outs),
        in_specs=[VM] * n_in,
        out_specs=(VM,) * len(outs),
        scratch_shapes=scratch,
        compiler_params=pltpu.CompilerParams(vmem_limit_bytes=60 << 20, **extra),
        name=name,
    )


def on_device(x, ws, w, bias, cot):
    v = lambda *s: pltpu.VMEM(s, BF)
    f = lambda *s: pltpu.VMEM(s, F32)
    l4, lt, rn = call(
        forward_kernel,
        [((16, 128, 128), BF), ((2048, 128), BF), ((32, 128, 128), BF)],
        2,
        [f(1024, 64), v(16, 16, 128), v(8, 32, 128), v(16, 16, 128), v(8, 32, 128), v(16, 8, 16, 128), v(32, 16, 8, 128)]
        + [DMA((16,)), DMA((16,)), DMA((8,)), DMA((8,)), DMA((7,)), DMA((8,)), DMA((15,)), DMA((16,))],
        "forward",
        0,
    )(x, ws)
    wr = w.reshape(32, 32, 128).swapaxes(0, 1).reshape(1024, 128)
    wt = wr.T
    pair, lg, rg, wg = call(
        middle_kernel,
        [((64, 128, 128), BF), ((16, 128, 128), BF), ((32, 8, 2, 8, 128), BF), ((16, 64, 128), BF)],
        7,
        [v(32, 2048, 128), v(32, 2048, 128)],
        "middle",
    )(l4, lt, rn, cot, wr, wt, bias.astype(F32).reshape(1, 128))
    grad, wout = call(
        backward_kernel,
        [((1, 1024, 64), BF), ((1024, 128), F32)],
        5,
        [f(1024, 64), v(32, 8, 8, 128), v(32, 8, 8, 128), v(3, 32, 2, 8, 128), v(32, 2, 8, 128), v(32, 8, 128), v(8, 32, 128), v(8, 32, 128)]
        + [v(3, 16, 32, 128), v(16, 2, 16, 128), v(16, 16, 128), v(16, 16, 128), v(16, 16, 128)]
        + [v(16, 64, 128), v(64, 128), v(8, 64, 128), v(16, 64, 128), f(1024, 128)]
        + [DMA((3,)), DMA((3,)), DMA((3,)), DMA((3,)), DMA((3,)), DMA((3,))]
        + [DMA((16,)), DMA((16,)), DMA((8,)), DMA((8,)), DMA((16,)), DMA((16,)), DMA((8,)), DMA((8,)), DMA((16,)), DMA((16,))],
        "backward",
        1,
    )(x, ws, lg, rg, wg)
    return pair, grad, wout


def solution(mesh):
    placed = (P(("row", "col"), None, None), P(), P(), P(), P("row", "col", None))
    return jax.shard_map(
        on_device,
        mesh=mesh,
        in_specs=placed,
        out_specs=(P("row", "col", None), P(("row", "col"), None, None), P()),
        check_vma=False,
    )
```

time: 428 us -> 97.6 us (0.23)
  waiting for transfers between devices: 199 us -> 0 us
  local copies, waits for them, and re-layouts: 96.1 us -> 7.24 us
  Pallas kernels: 0 us -> 87.8 us
  matrix products: 66.7 us -> 0 us
  starting transfers between devices: 41.1 us -> 0 us
  between operations: 14.4 us -> 0.67 us
  other arithmetic: 7.57 us -> 1.17 us
    psum x1 -> x0, waiting for transfers between devices: 145 us -> none  [on_device(): factor_weight_gradient = lax.psum(weight_part, ('row', 'col'))]
    pallas_call x0 -> x3, Pallas kernels: none -> 87.8 us  [the longest x1 32 us: on_device(): call(middle_kernel, [((64, 128, 128), BF), ((16, 128, 128), BF), ((32, 8,...]
    dot_general x26 -> x0, matrix products: 66.7 us -> none  [the longest x4 16.3 us: advance(): jnp.einsum('ijce,sic->sje', outer_grad, left_block, preferred_element_typ...]
    all_to_all x8 -> x0, waiting for transfers between devices: 53.5 us -> none  [the longest x2 21.3 us: summed_on_arrival(): pieces = lax.all_to_all(cut_along(array, dim, size), axis, 0, 0, tiled=True)]
    convert_element_type x10 -> x0, local copies, waits for them, and re-layouts: 44.2 us -> none  [the longest x4 26.1 us: advance(): jnp.dot(grad_rows, weight_back, preferred_element_type=jnp.float32)]
    all_to_all x8 -> x0, starting transfers between devices: 41.1 us -> none  [the longest x2 10.3 us: copy_for_each(): lax.all_to_all(jnp.broadcast_to(array[None], (size, *array.shape)), axis,...]
    while x69 -> x0, local copies, waits for them, and re-layouts: 18.8 us -> none
    unnamed x25 -> x5, local copies, waits for them, and re-layouts: 15.8 us -> 5.33 us
  transfers between devices with their start and end apart: 9 -> 0, of which waited for: 9 -> 0; matrix products, arithmetic and copies ran while one was open for 5% -> 0% of each run, Pallas kernels for 0% -> 0%
where the time goes in v1:
time: 97.6 us; the launch traced here: 96.8 us
  Pallas kernels  87.8 us (90%)
  local copies, waits for them, and re-layouts  7.24 us (7%)
  other arithmetic  1.17 us (1%)
    pallas_call x1, Pallas kernels, on_device(): call(middle_kernel, [((64, 128, 128), BF), ((16, 128, 128), BF), ((32, 8,...  32 us
    pallas_call x1, Pallas kernels, on_device(): call(backward_kernel, [((1, 1024, 64), BF), ((1024, 128), F32)], 5, [f(10...  28.9 us
    pallas_call x1, Pallas kernels, on_device(): call(forward_kernel, [((16, 128, 128), BF), ((2048, 128), BF), ((32, 128,...  26.9 us
    unnamed x5, local copies, waits for them, and re-layouts  5.33 us

profile of v1, /device:TPU:1, one launch (start us, length us, event | category | flops | bytes accessed | tf_op | source)
XLA Modules:
  0.0 96.8 jit_solution(9650473119496161809)
XLA Ops:
  0.6 1.2 %bitcast_convert_fusion.bias = f32[1,128]{1,0:T(1,128)} fusion(bf16[128]{0:T(256)(128)(2,1)} %param.8), kind=kLoop, calls=%fused_computation | loop fusion | flops 128 | bytes 768 | tf_op jit(solution)/shard_map/reshape | solution.py:469
  1.8 1.7 %copy.17.x = bf16[1,1024,64]{2,1,0:T(8,128)(2,1)} copy(bf16[1,1024,64]{1,2,0:T(8,128)(2,1)} %param.5) | data formatting | bytes 262144 | tf_op args[0]
  3.5 1.1 %copy.18 = bf16[32,32,128]{2,1,0:T(8,128)(2,1)S(1)} copy(bf16[32,32,128]{2,0,1:T(8,128)(2,1)} %bitcast.11) | data formatting | bytes 524288 | tf_op jit(solution)/shard_map/transpose | solution.py:461
  4.6 0.0 copy-start
  4.6 0.9 copy.19
  5.4 26.9 %forward.1 = (bf16[16,128,128]{2,1,0:T(8,128)(2,1)}, bf16[2048,128]{1,0:T(8,128)(2,1)}, bf16[32,128,128]{2,1,0:T(8,128)(2,1)}) custom-call(bf16[1,1024,64]{2,1,0:T(8,128)(2,1)} %copy.17.x, bf16[64,64]{1,0:T(8,128)(2,1)} %ws_ref.3), custom_call_target="tpu_custom_call" | custom-call | tf_op jit(solution)/shard_map/forward/pallas_call | solution.py:452
  32.4 0.0 copy-done
  32.4 32.0 %middle.1 = (bf16[64,128,128]{2,1,0:T(8,128)(2,1)}, bf16[16,128,128]{2,1,0:T(8,128)(2,1)}, bf16[32,8,2,8,128]{4,3,2,1,0:T(8,128)(2,1)}, bf16[16,64,128]{2,1,0:T(8,128)(2,1)}) custom-call(bf16[16,128,128]{2,1,0:T(8,128)(2,1)} %get-tuple-element.12.l4, bf16[2048,128]{1,0:T(8,128)(2,1)} %get-tuple-element.13.lt, bf16[32,128,128]{2,1,0:T(8,128)(2,1)} %get-tuple-element.14.rn, ...), custom_call_target="tpu_custom_call" | custom-call | tf_op jit(solution)/shard_map/middle/pallas_call | solution.py:463
  64.4 28.9 %backward.1 = (bf16[1,1024,64]{2,1,0:T(8,128)(2,1)}, f32[1024,128]{1,0:T(8,128)}) custom-call(bf16[1,1024,64]{2,1,0:T(8,128)(2,1)} %copy.17.x, bf16[64,64]{1,0:T(8,128)(2,1)} %ws_ref.3, bf16[16,128,128]{2,1,0:T(8,128)(2,1)} %get-tuple-element.16.lg, bf16[32,8,2,8,128]{4,3,2,1,0:T(8,128)(2,1)} %get-tuple-element.17.rg, bf16[16,64,128]{2,1,0:T(8,128)(2,1)} %get-tuple-element.18.wg), custom_call_target="tpu_custom_call" | custom-call | tf_op jit(solution)/shard_map/backward/pallas_call | solution.py:470
  93.2 1.7 %copy.21 = bf16[1,1024,64]{1,2,0:T(8,128)(2,1)} copy(bf16[1,1024,64]{2,1,0:T(8,128)(2,1)} %get-tuple-element.28) | data formatting | bytes 262144
  95.0 1.9 %copy.23 = f32[1024,128]{1,0:T(8,128)} copy(f32[1024,128]{1,0:T(8,128)} %get-tuple-element.35) | data formatting | bytes 1048576
Async XLA Ops:
  4.6 27.8 %copy-start = (bf16[32,32,128]{2,1,0:T(8,128)(2,1)}, bf16[32,32,128]{2,1,0:T(8,128)(2,1)S(1)}, u32[]{:S(2)}) copy-start(bf16[32,32,128]{2,1,0:T(8,128)(2,1)S(1)} %copy.18) | copy-start | bytes 786436

commit v2 on v1

v2 whole, which is shorter than its diff:
```python
import functools

import jax
import jax.numpy as jnp
from jax import lax
from jax.experimental import pallas as pl
from jax.experimental.pallas import tpu as pltpu
from jax.sharding import PartitionSpec as P

BF = jnp.bfloat16
F32 = jnp.float32
MESH = pl.DeviceIdType.MESH
NT = (((1,), (1,)), ((), ()))
DMA = pltpu.SemaphoreType.DMA


def dot(a, b):
    return jnp.dot(a, b, preferred_element_type=F32)


def dnt(a, b):
    return lax.dot_general(a, b, NT, preferred_element_type=F32)


def place():
    r, q = lax.axis_index("row"), lax.axis_index("col")
    y, zh, c = lax.div(r, 4), lax.rem(lax.div(r, 2), 2), lax.rem(r, 2)
    x, zl = lax.div(q, 2), lax.rem(q, 2)
    return r, q, y, zh, c, x, zl


def row_of(y, zh, c):
    return y * 4 + zh * 2 + c


def remote(src, dst, send, recv, to):
    return pltpu.make_async_remote_copy(
        src_ref=src, dst_ref=dst, send_sem=send, recv_sem=recv, device_id=to, device_id_type=MESH
    )


def greet(r, q):
    barrier = pltpu.get_barrier_semaphore()
    for d in range(1, 16):
        pl.semaphore_signal(barrier, inc=1, device_id=(lax.rem(r + d, 16), q), device_id_type=MESH)
    for d in range(1, 8):
        pl.semaphore_signal(barrier, inc=1, device_id=(r, lax.rem(q + d, 8)), device_id_type=MESH)


def greeted():
    pl.semaphore_wait(pltpu.get_barrier_semaphore(), 22)


def standardized(x_ref):
    x = x_ref[...].astype(F32)
    centred = x - jnp.mean(x, axis=0, keepdims=True)
    rstd = lax.rsqrt(jnp.mean(centred * centred, axis=0, keepdims=True) + 1e-5)
    return centred * rstd, rstd


def widened(ws, t):
    left = ws[:, :32]
    tiled = jnp.concatenate([left] * 4, axis=1)
    lane = lax.broadcasted_iota(jnp.int32, (64, 128), 1)
    return jnp.where(lane // 32 == t, tiled, 0.0).astype(BF)


def swapped(outer, inner):
    n = outer * inner
    to = lax.broadcasted_iota(jnp.int32, (n, n), 0)
    at = lax.broadcasted_iota(jnp.int32, (n, n), 1)
    return (at == (to % outer) * inner + to // outer).astype(F32).astype(BF)


def project(ws, xt, xs, lsend, rsend):
    right = ws.T[32:, :].astype(BF)
    for q in range(8):
        cols = xt[:, q * 128 : (q + 1) * 128]
        xs[q * 128 : (q + 1) * 128, :] = cols.T
        rsend[q] = dot(right, cols.astype(BF)).astype(BF)
    for t in range(4):
        part = xs[pl.ds(t, 256, stride=4), :].astype(BF)
        term = dot(part, widened(ws, t))
        acc = term if t == 0 else acc + term
    lsend[...] = acc.astype(BF).reshape(16, 16, 128)


def scatter_start(r, q, lsend, rsend, l1, r1, sems):
    ls, lr, rs, rr = sems
    out = []
    for d in range(1, 16):
        to = lax.rem(r + d, 16)
        cp = remote(lsend.at[to], l1.at[r], ls.at[d], lr.at[r], (to, q))
        cp.start()
        out.append(cp)
    for d in range(1, 8):
        to = lax.rem(q + d, 8)
        cp = remote(rsend.at[to], r1.at[q], rs.at[d], rr.at[q], (r, to))
        cp.start()
        out.append(cp)
    return out


def wait_row(r, q, buf, recv, send):
    for d in range(1, 16):
        at = lax.rem(r + d, 16)
        remote(buf.at[at], buf.at[at], send.at[d], recv.at[at], (at, q)).wait_recv()


def wait_col(r, q, buf, recv, send):
    for d in range(1, 8):
        at = lax.rem(q + d, 8)
        remote(buf.at[at], buf.at[at], send.at[d], recv.at[at], (r, at)).wait_recv()


class Sends:
    def __init__(self, buf, send, recv):
        self.buf, self.send, self.recv, self.n, self.all = buf, send, recv, 0, []

    def start(self, slot, to):
        ref = self.buf.at[:, slot]
        cp = remote(ref, ref, self.send.at[self.n], self.recv.at[slot], to)
        self.n += 1
        cp.start()
        self.all.append(cp)

    def arrived(self, slot, source):
        ref = self.buf.at[:, slot]
        remote(ref, ref, self.send.at[0], self.recv.at[slot], source).wait_recv()


def spread_left(p, sends):
    r, q, y, zh, c, x, zl = p
    over = x * 2 + 1 - zl
    sends.start(q, (r, over))
    for d in (1, 3, 2):
        sends.start(q, (r, lax.rem(x + d, 4) * 2 + zl))

    def relay():
        sends.arrived(over, (r, over))
        for d in (1, 3, 2):
            sends.start(over, (r, lax.rem(x + d, 4) * 2 + zl))

    def rest():
        for d in (1, 3, 2):
            xd = lax.rem(x + d, 4)
            sends.arrived(xd * 2 + zl, (r, xd * 2 + zl))
            sends.arrived(xd * 2 + 1 - zl, (r, xd * 2 + zl))

    return relay, rest


def spread_right(p, sends):
    r, q, y, zh, c, x, zl = p
    over = row_of(y, 1 - zh, c)
    mate = row_of(y, zh, 1 - c)
    sends.start(r, (over, q))
    for d in (1, 3, 2):
        sends.start(r, (row_of(lax.rem(y + d, 4), zh, c), q))
    sends.start(r, (mate, q))

    def relay():
        sends.arrived(over, (over, q))
        for d in (1, 3, 2):
            sends.start(over, (row_of(lax.rem(y + d, 4), zh, c), q))
        sends.start(over, (mate, q))

    def pass_on():
        for zz in (zh, 1 - zh):
            for d in (1, 3, 2):
                yd = lax.rem(y + d, 4)
                slot = row_of(yd, zz, c)
                sends.arrived(slot, (row_of(yd, zh, c), q))
                sends.start(slot, (mate, q))

    def rest():
        for zz in (zh, 1 - zh):
            for d in range(4):
                sends.arrived(row_of(lax.rem(y + d, 4), zz, 1 - c), (mate, q))

    return relay, pass_on, rest


def natural_left(l3, l4, lt):
    order = swapped(8, 16)
    for a in range(16):
        rows = dot(order, l3[a].reshape(128, 128)) * (1.0 / 128.0)
        l4[a] = rows.astype(BF)
        lt[a * 128 : (a + 1) * 128, :] = rows.T.astype(BF)


def steps(lo, hi, body):
    if hi - lo == 1:
        body(lo)
    else:
        pl.loop(lo, hi)(body)


def grad_outer(cot, wr, G, lo, hi, unroll=8):
    def body(step):
        for u in range(unroll):
            p = step * unroll + u
            o = dnt(wr[...], cot[pl.ds(2 * p, 2)].reshape(256, 128)).astype(BF)
            for h in range(2):
                G[:, pl.ds(pl.multiple_of((2 * p + h) * 32, 32), 32), :] = o[:, h * 128 : (h + 1) * 128].reshape(32, 32, 128)

    steps(lo, hi, body)


def outer_product(lt, R, O, lo, hi, unroll=4):
    def body(step):
        for u in range(unroll):
            p = step * unroll + u
            o = dot(lt[...], jnp.concatenate([R[2 * p], R[2 * p + 1]], axis=1)).astype(BF)
            O[2 * p] = o[:, :128]
            O[2 * p + 1] = o[:, 128:]

    steps(lo, hi, body)


def left_gradient(G, R, put, lo, hi, M=512):
    def body(m):
        rows = pl.ds(pl.multiple_of(m * M, M), M)
        for p in range(16):
            g = jnp.concatenate([G[2 * p, rows, :], G[2 * p + 1, rows, :]], axis=1)
            term = dnt(g, jnp.concatenate([R[2 * p], R[2 * p + 1]], axis=1))
            acc = term if p == 0 else acc + term
        put(m, acc * (1.0 / 128.0))

    steps(lo, hi, body)


def right_gradient(G, l4, put, lo, hi, unroll=8):
    def body(step):
        for u in range(unroll):
            p = step * unroll + u
            for k in range(8):
                rows = slice(k * 256, (k + 1) * 256)
                g = jnp.concatenate([G[2 * p, rows, :], G[2 * p + 1, rows, :]], axis=1)
                term = dot(jnp.concatenate([l4[2 * k], l4[2 * k + 1]], axis=1), g)
                acc = term if k == 0 else acc + term
            put(2 * p, acc[:, :128])
            put(2 * p + 1, acc[:, 128:])

    steps(lo, hi, body)


def weight_gradient(O, cot, put, lo, hi, E=8):
    def body(m):
        for p in range(32):
            x = jnp.concatenate(
                [O[pl.ds(m * E, E), (2 * p + h) * 32 : (2 * p + h + 1) * 32, :].reshape(E * 32, 128) for h in range(2)], axis=1
            )
            term = dot(x, cot[2 * p : 2 * p + 2].reshape(256, 128))
            acc = term if p == 0 else acc + term
        put(m, acc)

    steps(lo, hi, body)


def of_row(O, i):
    return O[:, pl.ds(pl.multiple_of(i * 32, 32), 32), :].reshape(1024, 128)


def pair_update(O, wt, bias, out, lo, hi, unroll=8):
    wide = bias[...].astype(F32)

    def body(step):
        for u in range(unroll):
            p = step * unroll + u
            y = dot(wt[...], jnp.concatenate([of_row(O, 2 * p), of_row(O, 2 * p + 1)], axis=1))
            for h in range(2):
                out[2 * p + h] = (y[:, h * 128 : (h + 1) * 128].T + wide).astype(BF)

    steps(lo, hi, body)


def to_row(p, src, dst, send, recv):
    r, q = p[0], p[1]
    out = []
    for d in range(1, 16):
        to = lax.rem(r + d, 16)
        cp = remote(src(to), dst.at[r], send.at[d], recv.at[r], (to, q))
        cp.start()
        out.append(cp)
    return out


def to_col(p, src, dst, send, recv):
    r, q = p[0], p[1]
    out = []
    for d in range(1, 8):
        to = lax.rem(q + d, 8)
        cp = remote(src(to), dst.at[q], send.at[d], recv.at[q], (r, to))
        cp.start()
        out.append(cp)
    return out


def summed(buf, n):
    acc = buf[0].astype(F32)
    for k in range(1, n):
        acc = acc + buf[k].astype(F32)
    return acc


def whole_kernel(
    x, ws_ref, w, bias, cot_hbm, pair_hbm, grad, wout,
    xt, xs, wf, wr, wt, cot, pair, G, O,
    lsend, rsend, l1, r1, l3, r3, rn, l4, lt,
    rg, rc, rcs, ry, rys, rz, r6, rin, lg, lx, lxs, lz, l6, lin,
    wg, wgot, wsum, wc, wall,
    cot_sem, pair_sem,
    ls, lr, rs, rr, l2s, l2r, r2s, r2r,
    cs, cr, ys, yr, xs_s, xs_r, zs, zr, lo_s, lo_r, ro_s, ro_r, w1s, w1r, w2s, w2r, w3s, w3r,
):
    p = place()
    r, q, y, zh, c, xx, zl = p
    mate = (row_of(y, zh, 1 - c), q)
    greet(r, q)
    cot_copy = pltpu.make_async_copy(cot_hbm, cot, cot_sem.at[0])
    cot_copy.start()
    ws = ws_ref[...].astype(F32)
    xhat, rstd = standardized(x)
    xt[...] = xhat
    project(ws, xt, xs, lsend, rsend)
    l1[r] = lsend[r]
    r1[q] = rsend[q]
    greeted()
    sent = scatter_start(r, q, lsend, rsend, l1, r1, (ls, lr, rs, rr))
    wf[...] = w[...].astype(F32)
    for e in range(32):
        wr[e * 32 : (e + 1) * 32, :] = wf[pl.ds(e, 32, stride=32), :].astype(BF)
    for k in range(8):
        wt[:, k * 128 : (k + 1) * 128] = wr[k * 128 : (k + 1) * 128, :].astype(F32).T.astype(BF)
    left_order, right_order = swapped(16, 16), swapped(8, 32)
    cot_copy.wait()
    grad_outer(cot, wr, G, 0, 2)
    wait_col(r, q, r1, rr, rs)
    r3[:, r] = dot(right_order, r1[...].reshape(256, 128)).reshape(32, 8, 128).astype(BF)
    rsends = Sends(r3, r2s, r2r)
    rrelay, rpass, rrest = spread_right(p, rsends)
    wait_row(r, q, l1, lr, ls)
    l3[:, q] = dot(left_order, l1[...].reshape(256, 128)).astype(BF).reshape(16, 16, 128)
    lsends = Sends(l3, l2s, l2r)
    lrelay, lrest = spread_left(p, lsends)
    grad_outer(cot, wr, G, 2, 3)
    rrelay()
    lrelay()
    grad_outer(cot, wr, G, 3, 4)
    lrest()
    natural_left(l3, l4, lt)
    rpass()

    def put_right(e, v):
        rg[e] = v.reshape(8, 2, 8, 128).astype(BF)

    core = []
    for half in range(2):
        right_gradient(G, l4, put_right, half, half + 1)
        es = pl.ds(half * 16, 16)
        cp = remote(rg.at[es, :, 1 - c], rc.at[es], cs.at[half], cr.at[half], mate)
        cp.start()
        core.append(cp)
    rrest()
    for e in range(32):
        rn[e] = r3[e].reshape(128, 128)

    def put_weight(m, v):
        wg[m * 4 : (m + 1) * 4] = v.astype(BF).reshape(4, 64, 128)

    ycp = []
    for m in range(4):
        outer_product(lt, rn, O, m, m + 1)
        weight_gradient(O, cot, put_weight, m, m + 1)
        for k in range(4 * m, 4 * m + 4):
            @pl.when(r != k)
            def _():
                remote(wg.at[k], wgot.at[r], w1s.at[k], w1r.at[r], (k, q)).start()

        if m == 0:
            for cp in core:
                cp.wait_recv()
            for e in range(32):
                rcs[e] = (rg[e, :, c].astype(F32) + rc[e].astype(F32)).astype(BF)
            for d in (1, 3, 2):
                to = lax.rem(y + d, 4)
                cp = remote(rcs.at[:, pl.ds(to * 2, 2)], ry.at[d - 1], ys.at[d - 1], yr.at[d - 1], (row_of(to, zh, c), q))
                cp.start()
                ycp.append(cp)
    wgot[r] = wg[r]

    def put_left(m, v):
        v = v.astype(BF)
        for k in range(4):
            lg[m * 4 + k] = dnt(swapped(16, 8), v[k * 128 : (k + 1) * 128, :]).astype(BF)

    xcp = []
    one = []
    for m in range(4):
        left_gradient(G, rn, put_left, m, m + 1)
        rows = pl.ds(m * 4, 4)
        for d in (1, 3, 2):
            to = lax.rem(xx + d, 4)
            at = (d - 1) * 4 + m
            cp = remote(lg.at[rows, pl.ds(to * 32, 32), :], lx.at[d - 1, rows], xs_s.at[at], xs_r.at[at], (r, to * 2 + zl))
            cp.start()
            xcp.append(cp)
        if m == 0:
            for cp in ycp:
                cp.wait_recv()
            for e in range(32):
                own = rcs[e, pl.ds(y * 2, 2)].astype(F32)
                for d in range(3):
                    own = own + ry[d, e].astype(F32)
                rys[e] = own.astype(BF)
            rzc = remote(rys.at[:, 1 - zh], rz, zs.at[0], zr.at[0], (row_of(y, 1 - zh, c), q))
            rzc.start()
            one.append(rzc)
        if m == 1:
            wait_row(r, q, wgot, w1r, w1s)
            wsum[...] = summed(wgot, 16).astype(BF)
            wc[q] = wsum[...]
            sent += to_col(p, lambda to: wsum, wc, w2s, w2r)
        if m == 3:
            rzc.wait_recv()
            five = rys[:, zh].astype(F32) + rz[...].astype(F32)
            r6[...] = dot(swapped(32, 8), five.reshape(256, 128).astype(BF)).astype(BF).reshape(8, 32, 128)
            rin[q] = r6[q]
            sent += to_col(p, lambda to: r6.at[to], rin, ro_s, ro_r)
    wait_col(r, q, wc, w2r, w2s)
    wall[r] = summed(wc, 8).astype(BF)
    sent += to_row(p, lambda to: wall.at[r], wall, w3s, w3r)

    pcp = []
    for half in range(2):
        pair_update(O, wt, bias, pair, 2 * half, 2 * half + 2)
        rows = pl.ds(half * 32, 32)
        cp = pltpu.make_async_copy(pair.at[rows], pair_hbm.at[rows], pair_sem.at[half])
        cp.start()
        pcp.append(cp)
        if half == 0:
            for cp in xcp:
                cp.wait_recv()
            for a in range(16):
                own = lg[a, pl.ds(pl.multiple_of(xx * 32, 32), 32), :].astype(F32)
                for d in range(3):
                    own = own + lx[d, a].astype(F32)
                lxs[a] = own.astype(BF).reshape(2, 16, 128)
            lzc = remote(lxs.at[:, 1 - zl], lz, zs.at[1], zr.at[1], (r, xx * 2 + 1 - zl))
            lzc.start()
            one.append(lzc)
    lzc.wait_recv()
    five = (lxs[:, zl].astype(F32) + lz[...].astype(F32)).astype(BF)
    l6[...] = dot(swapped(16, 16), five.reshape(256, 128)).astype(BF).reshape(16, 16, 128)
    lin[r] = l6[r]
    sent += to_row(p, lambda to: l6.at[to], lin, lo_s, lo_r)
    wait_row(r, q, wall, w3r, w3s)
    for k in range(16):
        wf[k * 64 : (k + 1) * 64, :] = wall[k].astype(F32)
    for k in range(32):
        wout[k * 32 : (k + 1) * 32, :] = wf[pl.ds(k, 32, stride=32), :]
    wait_col(r, q, rin, ro_r, ro_s)
    wait_row(r, q, lin, lo_r, lo_s)
    flat = lin[...].reshape(256, 128)
    for t in range(4):
        xs[pl.ds(t, 256, stride=4), :] = dnt(flat, widened(ws, t))
    right = ws[:, 32:].astype(BF)
    for k in range(8):
        cols = slice(k * 128, (k + 1) * 128)
        ng = dot(right, rin[k]) + xs[cols, :].T
        xh = xt[:, cols]
        first = jnp.mean(ng, axis=0, keepdims=True)
        second = jnp.mean(ng * xh, axis=0, keepdims=True)
        grad[:, cols] = (rstd[:, cols] * (ng - first - xh * second)).astype(BF)
    for cp in sent + rsends.all + lsends.all + core + ycp + xcp + one:
        cp.wait_send()
    for k in range(16):
        @pl.when(r != k)
        def _():
            remote(wg.at[k], wgot.at[r], w1s.at[k], w1r.at[r], (k, q)).wait_send()

    for cp in pcp:
        cp.wait()


VM = pl.BlockSpec(memory_space=pltpu.VMEM)
ANY = pl.BlockSpec(memory_space=pl.ANY)


def on_device(x, ws, w, bias, cot):
    v = lambda *s: pltpu.VMEM(s, BF)
    f = lambda *s: pltpu.VMEM(s, F32)
    pair, grad, wout = pl.pallas_call(
        whole_kernel,
        out_shape=(
            jax.ShapeDtypeStruct((64, 128, 128), BF),
            jax.ShapeDtypeStruct((64, 1024), BF),
            jax.ShapeDtypeStruct((1024, 128), F32),
        ),
        in_specs=[VM, VM, VM, VM, ANY],
        out_specs=(ANY, VM, VM),
        scratch_shapes=[f(64, 1024), f(1024, 64), f(1024, 128), v(1024, 128), v(128, 1024), v(64, 128, 128), v(64, 128, 128)]
        + [v(32, 2048, 128), v(32, 2048, 128)]
        + [v(16, 16, 128), v(8, 32, 128), v(16, 16, 128), v(8, 32, 128), v(16, 8, 16, 128), v(32, 16, 8, 128), v(32, 128, 128)]
        + [v(16, 128, 128), v(2048, 128)]
        + [v(32, 8, 2, 8, 128), v(32, 8, 8, 128), v(32, 8, 8, 128), v(3, 32, 2, 8, 128), v(32, 2, 8, 128), v(32, 8, 128)]
        + [v(8, 32, 128), v(8, 32, 128)]
        + [v(16, 128, 128), v(3, 16, 32, 128), v(16, 2, 16, 128), v(16, 16, 128), v(16, 16, 128), v(16, 16, 128)]
        + [v(16, 64, 128), v(16, 64, 128), v(64, 128), v(8, 64, 128), v(16, 64, 128)]
        + [DMA((1,)), DMA((2,))]
        + [DMA((16,)), DMA((16,)), DMA((8,)), DMA((8,)), DMA((7,)), DMA((8,)), DMA((15,)), DMA((16,))]
        + [DMA((2,)), DMA((2,)), DMA((3,)), DMA((3,)), DMA((12,)), DMA((12,)), DMA((2,)), DMA((2,))]
        + [DMA((16,)), DMA((16,)), DMA((8,)), DMA((8,)), DMA((16,)), DMA((16,)), DMA((8,)), DMA((8,)), DMA((16,)), DMA((16,))],
        compiler_params=pltpu.CompilerParams(vmem_limit_bytes=60 << 20, collective_id=0, has_side_effects=True),
        name="whole",
    )(x[0].T, ws, w, bias.reshape(1, 128), cot)
    return pair, grad.T[None], wout


def solution(mesh):
    placed = (P(("row", "col"), None, None), P(), P(), P(), P("row", "col", None))
    return jax.shard_map(
        on_device,
        mesh=mesh,
        in_specs=placed,
        out_specs=(P("row", "col", None), P(("row", "col"), None, None), P()),
        check_vma=False,
    )
```

time: 97.6 us -> 69.8 us (0.72)
  Pallas kernels: 87.8 us -> 64.3 us
  local copies, waits for them, and re-layouts: 7.24 us -> 4.68 us
  other arithmetic: 1.17 us -> 0 us
    pallas_call x3 -> x1, Pallas kernels: 87.8 us -> 64.3 us  [on_device(): pl.pallas_call(whole_kernel, out_shape=(jax.ShapeDtypeStruct((64, 128, 12...]
    reshape x1 -> x0, other arithmetic: 1.17 us -> none  [on_device(): bias.astype(F32).reshape(1, 128)]
    transpose x1 -> x0, local copies, waits for them, and re-layouts: 1.05 us -> none  [on_device(): wr = w.reshape(32, 32, 128).swapaxes(0, 1).reshape(1024, 128)]
    unnamed x5 -> x7, local copies, waits for them, and re-layouts: 5.33 us -> 4.68 us
where the time goes in v2:
time: 69.8 us; the launch traced here: 69.6 us
  Pallas kernels  64.3 us (92%)
  local copies, waits for them, and re-layouts  4.68 us (7%)
    pallas_call x1, Pallas kernels, on_device(): pl.pallas_call(whole_kernel, out_shape=(jax.ShapeDtypeStruct((64, 128, 12...  64.3 us
    unnamed x7, local copies, waits for them, and re-layouts  4.68 us

profile of v2, /device:TPU:1, one launch (start us, length us, event | category | flops | bytes accessed | tf_op | source)
XLA Modules:
  0.0 69.6 jit_solution(15207613381885940655)
XLA Ops:
  0.6 64.3 %whole.1 = (bf16[64,128,128]{2,1,0:T(8,128)(2,1)}, bf16[64,1024]{1,0:T(8,128)(2,1)}, f32[1024,128]{1,0:T(8,128)}) custom-call(bf16[64,1024]{1,0:T(8,128)(2,1)} %bitcast.7, bf16[64,64]{1,0:T(8,128)(2,1)} %ws_ref.1, bf16[1024,128]{1,0:T(8,128)(2,1)} %w.1, bf16[1,128]{1,0:T(2,128)(2,1)} %bitcast.9, bf16[64,128,128]{2,1,0:T(8,128)(2,1)} %cot_hbm.1), custom_call_target="tpu_custom_call" | custom-call | tf_op jit(solution)/shard_map/whole/pallas_call | solution.py:494
  64.9 0.0 copy-start.1
  64.9 0.0 copy-start
  64.9 3.2 %copy.11 = bf16[64,128,128]{2,1,0:T(8,128)(2,1)} copy(bf16[64,128,128]{2,1,0:T(8,128)(2,1)} %get-tuple-element.12) | data formatting | bytes 4194304
  68.2 0.0 copy-done.1
  68.2 0.7 copy.12
  68.8 0.0 copy-done
  68.8 0.8 %copy.13 = f32[1024,128]{1,0:T(8,128)} copy(f32[1024,128]{1,0:T(8,128)S(1)} %copy-done) | data formatting | bytes 1048576
Async XLA Ops:
  64.9 3.2 %copy-start.1 = (bf16[64,1024]{1,0:T(8,128)(2,1)S(1)}, bf16[64,1024]{1,0:T(8,128)(2,1)}, u32[]{:S(2)}) copy-start(bf16[64,1024]{1,0:T(8,128)(2,1)} %get-tuple-element.7) | copy-start | bytes 393220
  64.9 3.9 %copy-start = (f32[1024,128]{1,0:T(8,128)S(1)}, f32[1024,128]{1,0:T(8,128)}, u32[]{:S(2)}) copy-start(f32[1024,128]{1,0:T(8,128)} %get-tuple-element.14) | copy-start | bytes 1572868

commit v3 on v2

--- a/solution.py
+++ b/solution.py
@@ -207,27 +207,21 @@
     steps(lo, hi, body)
 
 
-def outer_product(lt, R, O, lo, hi, unroll=4):
-    def body(step):
-        for u in range(unroll):
-            p = step * unroll + u
-            o = dot(lt[...], jnp.concatenate([R[2 * p], R[2 * p + 1]], axis=1)).astype(BF)
-            O[2 * p] = o[:, :128]
-            O[2 * p + 1] = o[:, 128:]
-
-    steps(lo, hi, body)
-
-
-def left_gradient(G, R, put, lo, hi, M=512):
-    def body(m):
-        rows = pl.ds(pl.multiple_of(m * M, M), M)
-        for p in range(16):
-            g = jnp.concatenate([G[2 * p, rows, :], G[2 * p + 1, rows, :]], axis=1)
-            term = dnt(g, jnp.concatenate([R[2 * p], R[2 * p + 1]], axis=1))
-            acc = term if p == 0 else acc + term
-        put(m, acc * (1.0 / 128.0))
-
-    steps(lo, hi, body)
+def outer_product(lt, R, O, at, m):
+    for u in range(4):
+        p = m * 4 + u
+        o = dot(lt[...], jnp.concatenate([R[2 * p], R[2 * p + 1]], axis=1)).astype(BF)
+        O[8 * at + 2 * u] = o[:, :128]
+        O[8 * at + 2 * u + 1] = o[:, 128:]
+
+
+def left_gradient(G, R, m, M=512):
+    rows = slice(m * M, (m + 1) * M)
+    for p in range(16):
+        g = jnp.concatenate([G[2 * p, rows, :], G[2 * p + 1, rows, :]], axis=1)
+        term = dnt(g, jnp.concatenate([R[2 * p], R[2 * p + 1]], axis=1))
+        acc = term if p == 0 else acc + term
+    return acc * (1.0 / 128.0)
 
 
 def right_gradient(G, l4, put, lo, hi, unroll=8):
@@ -245,17 +239,14 @@
     steps(lo, hi, body)
 
 
-def weight_gradient(O, cot, put, lo, hi, E=8):
-    def body(m):
-        for p in range(32):
-            x = jnp.concatenate(
-                [O[pl.ds(m * E, E), (2 * p + h) * 32 : (2 * p + h + 1) * 32, :].reshape(E * 32, 128) for h in range(2)], axis=1
-            )
-            term = dot(x, cot[2 * p : 2 * p + 2].reshape(256, 128))
-            acc = term if p == 0 else acc + term
-        put(m, acc)
-
-    steps(lo, hi, body)
+def weight_gradient(O, cot, at):
+    for p in range(32):
+        x = jnp.concatenate(
+            [O[8 * at : 8 * at + 8, (2 * p + h) * 32 : (2 * p + h + 1) * 32, :].reshape(256, 128) for h in range(2)], axis=1
+        )
+        term = dot(x, cot[2 * p : 2 * p + 2].reshape(256, 128))
+        acc = term if p == 0 else acc + term
+    return acc
 
 
 def of_row(O, i):
@@ -305,12 +296,12 @@
 
 
 def whole_kernel(
-    x, ws_ref, w, bias, cot_hbm, pair_hbm, grad, wout,
-    xt, xs, wf, wr, wt, cot, pair, G, O,
+    x, ws_ref, w, bias, cot_hbm, pair, grad, wall,
+    xt, xs, wf, wr, wt, cot, G, O, raw, order,
     lsend, rsend, l1, r1, l3, r3, rn, l4, lt,
-    rg, rc, rcs, ry, rys, rz, r6, rin, lg, lx, lxs, lz, l6, lin,
-    wg, wgot, wsum, wc, wall,
-    cot_sem, pair_sem,
+    rg, rc, rcs, ry, rys, rz, r6, rin, lg, lx, l6, lin,
+    wg, wgot, wsum, wc,
+    cot_sem,
     ls, lr, rs, rr, l2s, l2r, r2s, r2r,
     cs, cr, ys, yr, xs_s, xs_r, zs, zr, lo_s, lo_r, ro_s, ro_r, w1s, w1r, w2s, w2r, w3s, w3r,
 ):
@@ -331,8 +322,11 @@
     wf[...] = w[...].astype(F32)
     for e in range(32):
         wr[e * 32 : (e + 1) * 32, :] = wf[pl.ds(e, 32, stride=32), :].astype(BF)
+    chunk = [lax.rem(y + d, 4) for d in (2, 1, 3, 0)]
     for k in range(8):
-        wt[:, k * 128 : (k + 1) * 128] = wr[k * 128 : (k + 1) * 128, :].astype(F32).T.astype(BF)
+        rows = pl.ds(pl.multiple_of(chunk[k // 2] * 256 + (k % 2) * 128, 128), 128)
+        wt[:, k * 128 : (k + 1) * 128] = wr[rows, :].astype(F32).T.astype(BF)
+    order[...] = swapped(16, 8)
     left_order, right_order = swapped(16, 16), swapped(8, 32)
     cot_copy.wait()
     grad_outer(cot, wr, G, 0, 2)
@@ -366,19 +360,12 @@
     for e in range(32):
         rn[e] = r3[e].reshape(128, 128)
 
-    def put_weight(m, v):
-        wg[m * 4 : (m + 1) * 4] = v.astype(BF).reshape(4, 64, 128)
-
-    ycp = []
-    for m in range(4):
-        outer_product(lt, rn, O, m, m + 1)
-        weight_gradient(O, cot, put_weight, m, m + 1)
-        for k in range(4 * m, 4 * m + 4):
-            @pl.when(r != k)
-            def _():
-                remote(wg.at[k], wgot.at[r], w1s.at[k], w1r.at[r], (k, q)).start()
-
-        if m == 0:
+    ycp, xcp, one = [], [], []
+    outer_product(lt, rn, O, 0, chunk[0])
+    for at in range(4):
+        if at < 3:
+            outer_product(lt, rn, O, at + 1, chunk[at + 1])
+        if at == 0:
             for cp in core:
                 cp.wait_recv()
             for e in range(32):
@@ -388,24 +375,32 @@
                 cp = remote(rcs.at[:, pl.ds(to * 2, 2)], ry.at[d - 1], ys.at[d - 1], yr.at[d - 1], (row_of(to, zh, c), q))
                 cp.start()
                 ycp.append(cp)
-    wgot[r] = wg[r]
-
-    def put_left(m, v):
-        v = v.astype(BF)
-        for k in range(4):
-            lg[m * 4 + k] = dnt(swapped(16, 8), v[k * 128 : (k + 1) * 128, :]).astype(BF)
-
-    xcp = []
-    one = []
+        wg[4 * at : 4 * at + 4] = weight_gradient(O, cot, at).astype(BF).reshape(4, 64, 128)
+        for k in range(4 if at < 3 else 3):
+            piece = k if at < 3 else lax.rem(zh * 2 + c + k + 1, 4)
+            sem = w1s.at[4 * at + k]
+            cp = remote(wg.at[4 * at + piece], wgot.at[r], sem, w1r.at[r], (chunk[at] * 4 + piece, q))
+            cp.start()
+            sent.append(cp)
+    wgot[r] = wg[12 + zh * 2 + c]
+
+    def put_left(m):
+        for k in range(4 * m, 4 * m + 4):
+            lg[k] = dnt(order[...], raw[k * 128 : (k + 1) * 128, :]).astype(BF)
+        rows = pl.ds(m * 4, 4)
+        for d in (4, 5, 3, 6, 2, 7, 1):
+            to = lax.rem(q + d, 8)
+            at = (d - 1) * 4 + m
+            src = lg.at[rows, pl.ds(pl.multiple_of(to * 16, 16), 16), :]
+            cp = remote(src, lx.at[q, rows], xs_s.at[at], xs_r.at[q * 4 + m], (r, to))
+            cp.start()
+            sent.append(cp)
+
     for m in range(4):
-        left_gradient(G, rn, put_left, m, m + 1)
-        rows = pl.ds(m * 4, 4)
-        for d in (1, 3, 2):
-            to = lax.rem(xx + d, 4)
-            at = (d - 1) * 4 + m
-            cp = remote(lg.at[rows, pl.ds(to * 32, 32), :], lx.at[d - 1, rows], xs_s.at[at], xs_r.at[at], (r, to * 2 + zl))
-            cp.start()
-            xcp.append(cp)
+        block = left_gradient(G, rn, m).astype(BF)
+        if m > 0:
+            put_left(m - 1)
+        raw[m * 512 : (m + 1) * 512, :] = block
         if m == 0:
             for cp in ycp:
                 cp.wait_recv()
@@ -417,49 +412,34 @@
             rzc = remote(rys.at[:, 1 - zh], rz, zs.at[0], zr.at[0], (row_of(y, 1 - zh, c), q))
             rzc.start()
             one.append(rzc)
-        if m == 1:
-            wait_row(r, q, wgot, w1r, w1s)
-            wsum[...] = summed(wgot, 16).astype(BF)
-            wc[q] = wsum[...]
-            sent += to_col(p, lambda to: wsum, wc, w2s, w2r)
-        if m == 3:
-            rzc.wait_recv()
-            five = rys[:, zh].astype(F32) + rz[...].astype(F32)
-            r6[...] = dot(swapped(32, 8), five.reshape(256, 128).astype(BF)).astype(BF).reshape(8, 32, 128)
-            rin[q] = r6[q]
-            sent += to_col(p, lambda to: r6.at[to], rin, ro_s, ro_r)
+    put_left(3)
+    wait_row(r, q, wgot, w1r, w1s)
+    wsum[...] = summed(wgot, 16).astype(BF)
+    wc[q] = wsum[...]
+    sent += to_col(p, lambda to: wsum, wc, w2s, w2r)
+    rzc.wait_recv()
+    five = rys[:, zh].astype(F32) + rz[...].astype(F32)
+    r6[...] = dot(swapped(32, 8), five.reshape(256, 128).astype(BF)).astype(BF).reshape(8, 32, 128)
+    rin[q] = r6[q]
+    sent += to_col(p, lambda to: r6.at[to], rin, ro_s, ro_r)
+    order2 = swapped(16, 16)
+
+    pair_update(O, wt, bias, pair, 0, 4)
+
     wait_col(r, q, wc, w2r, w2s)
     wall[r] = summed(wc, 8).astype(BF)
     sent += to_row(p, lambda to: wall.at[r], wall, w3s, w3r)
-
-    pcp = []
-    for half in range(2):
-        pair_update(O, wt, bias, pair, 2 * half, 2 * half + 2)
-        rows = pl.ds(half * 32, 32)
-        cp = pltpu.make_async_copy(pair.at[rows], pair_hbm.at[rows], pair_sem.at[half])
-        cp.start()
-        pcp.append(cp)
-        if half == 0:
-            for cp in xcp:
-                cp.wait_recv()
-            for a in range(16):
-                own = lg[a, pl.ds(pl.multiple_of(xx * 32, 32), 32), :].astype(F32)
-                for d in range(3):
-                    own = own + lx[d, a].astype(F32)
-                lxs[a] = own.astype(BF).reshape(2, 16, 128)
-            lzc = remote(lxs.at[:, 1 - zl], lz, zs.at[1], zr.at[1], (r, xx * 2 + 1 - zl))
-            lzc.start()
-            one.append(lzc)
-    lzc.wait_recv()
-    five = (lxs[:, zl].astype(F32) + lz[...].astype(F32)).astype(BF)
-    l6[...] = dot(swapped(16, 16), five.reshape(256, 128)).astype(BF).reshape(16, 16, 128)
+    for d in range(1, 8):
+        at = lax.rem(q + d, 8)
+        for m in range(4):
+            ref = lx.at[at, pl.ds(m * 4, 4)]
+            remote(ref, ref, xs_s.at[0], xs_r.at[at * 4 + m], (r, at)).wait_recv()
+    lx[q] = lg[:, pl.ds(pl.multiple_of(q * 16, 16), 16), :]
+    five = summed(lx, 8).astype(BF)
+    l6[...] = dot(order2, five.reshape(256, 128)).astype(BF).reshape(16, 16, 128)
     lin[r] = l6[r]
     sent += to_row(p, lambda to: l6.at[to], lin, lo_s, lo_r)
     wait_row(r, q, wall, w3r, w3s)
-    for k in range(16):
-        wf[k * 64 : (k + 1) * 64, :] = wall[k].astype(F32)
-    for k in range(32):
-        wout[k * 32 : (k + 1) * 32, :] = wf[pl.ds(k, 32, stride=32), :]
     wait_col(r, q, rin, ro_r, ro_s)
     wait_row(r, q, lin, lo_r, lo_s)
     flat = lin[...].reshape(256, 128)
@@ -475,12 +455,20 @@
         grad[:, cols] = (rstd[:, cols] * (ng - first - xh * second)).astype(BF)
     for cp in sent + rsends.all + lsends.all + core + ycp + xcp + one:
         cp.wait_send()
+
+
+def finish_kernel(pair, grad, wall, pair_out, grad_out, wout, wf, sems):
+    cps = [
+        pltpu.make_async_copy(pair, pair_out, sems.at[0]),
+        pltpu.make_async_copy(grad, grad_out, sems.at[1]),
+    ]
+    for cp in cps:
+        cp.start()
     for k in range(16):
-        @pl.when(r != k)
-        def _():
-            remote(wg.at[k], wgot.at[r], w1s.at[k], w1r.at[r], (k, q)).wait_send()
-
-    for cp in pcp:
+        wf[k * 64 : (k + 1) * 64, :] = wall[k].astype(F32)
+    for k in range(32):
+        wout[k * 32 : (k + 1) * 32, :] = wf[pl.ds(k, 32, stride=32), :]
+    for cp in cps:
         cp.wait()
 
 
@@ -491,30 +479,39 @@
 def on_device(x, ws, w, bias, cot):
     v = lambda *s: pltpu.VMEM(s, BF)
     f = lambda *s: pltpu.VMEM(s, F32)
+    pair, grad, wall = pl.pallas_call(
+        whole_kernel,
+        out_shape=(v(64, 128, 128), v(64, 1024), v(16, 64, 128)),
+        in_specs=[VM, VM, VM, VM, ANY],
+        out_specs=(VM, VM, VM),
+        scratch_shapes=[f(64, 1024), f(1024, 64), f(1024, 128), v(1024, 128), v(128, 1024), v(64, 128, 128)]
+        + [v(32, 2048, 128), v(32, 2048, 128), v(2048, 128), v(128, 128)]
+        + [v(16, 16, 128), v(8, 32, 128), v(16, 16, 128), v(8, 32, 128), v(16, 8, 16, 128), v(32, 16, 8, 128), v(32, 128, 128)]
+        + [v(16, 128, 128), v(2048, 128)]
+        + [v(32, 8, 2, 8, 128), v(32, 8, 8, 128), v(32, 8, 8, 128), v(3, 32, 2, 8, 128), v(32, 2, 8, 128), v(32, 8, 128)]
+        + [v(8, 32, 128), v(8, 32, 128)]
+        + [v(16, 128, 128), v(8, 16, 16, 128), v(16, 16, 128), v(16, 16, 128)]
+        + [v(16, 64, 128), v(16, 64, 128), v(64, 128), v(8, 64, 128)]
+        + [DMA((1,))]
+        + [DMA((16,)), DMA((16,)), DMA((8,)), DMA((8,)), DMA((7,)), DMA((8,)), DMA((15,)), DMA((16,))]
+        + [DMA((2,)), DMA((2,)), DMA((3,)), DMA((3,)), DMA((28,)), DMA((32,)), DMA((1,)), DMA((1,))]
+        + [DMA((16,)), DMA((16,)), DMA((8,)), DMA((8,)), DMA((16,)), DMA((16,)), DMA((8,)), DMA((8,)), DMA((16,)), DMA((16,))],
+        compiler_params=pltpu.CompilerParams(vmem_limit_bytes=54 << 20, collective_id=0, has_side_effects=True),
+        name="whole",
+    )(x[0].T, ws, w, bias.reshape(1, 128), cot)
     pair, grad, wout = pl.pallas_call(
-        whole_kernel,
+        finish_kernel,
         out_shape=(
             jax.ShapeDtypeStruct((64, 128, 128), BF),
             jax.ShapeDtypeStruct((64, 1024), BF),
             jax.ShapeDtypeStruct((1024, 128), F32),
         ),
-        in_specs=[VM, VM, VM, VM, ANY],
-        out_specs=(ANY, VM, VM),
-        scratch_shapes=[f(64, 1024), f(1024, 64), f(1024, 128), v(1024, 128), v(128, 1024), v(64, 128, 128), v(64, 128, 128)]
-        + [v(32, 2048, 128), v(32, 2048, 128)]
-        + [v(16, 16, 128), v(8, 32, 128), v(16, 16, 128), v(8, 32, 128), v(16, 8, 16, 128), v(32, 16, 8, 128), v(32, 128, 128)]
-        + [v(16, 128, 128), v(2048, 128)]
-        + [v(32, 8, 2, 8, 128), v(32, 8, 8, 128), v(32, 8, 8, 128), v(3, 32, 2, 8, 128), v(32, 2, 8, 128), v(32, 8, 128)]
-        + [v(8, 32, 128), v(8, 32, 128)]
-        + [v(16, 128, 128), v(3, 16, 32, 128), v(16, 2, 16, 128), v(16, 16, 128), v(16, 16, 128), v(16, 16, 128)]
-        + [v(16, 64, 128), v(16, 64, 128), v(64, 128), v(8, 64, 128), v(16, 64, 128)]
-        + [DMA((1,)), DMA((2,))]
-        + [DMA((16,)), DMA((16,)), DMA((8,)), DMA((8,)), DMA((7,)), DMA((8,)), DMA((15,)), DMA((16,))]
-        + [DMA((2,)), DMA((2,)), DMA((3,)), DMA((3,)), DMA((12,)), DMA((12,)), DMA((2,)), DMA((2,))]
-        + [DMA((16,)), DMA((16,)), DMA((8,)), DMA((8,)), DMA((16,)), DMA((16,)), DMA((8,)), DMA((8,)), DMA((16,)), DMA((16,))],
-        compiler_params=pltpu.CompilerParams(vmem_limit_bytes=60 << 20, collective_id=0, has_side_effects=True),
-        name="whole",
-    )(x[0].T, ws, w, bias.reshape(1, 128), cot)
+        in_specs=[VM, VM, VM],
+        out_specs=(ANY, ANY, VM),
+        scratch_shapes=[f(1024, 128), DMA((2,))],
+        compiler_params=pltpu.CompilerParams(vmem_limit_bytes=8 << 20),
+        name="finish",
+    )(pair, grad, wall)
     return pair, grad.T[None], wout
 
 

time: 69.8 us -> 63.8 us (0.914)
  local copies, waits for them, and re-layouts: 4.68 us -> 0 us
  Pallas kernels: 64.3 us -> 62.8 us
    unnamed x7 -> x0, local copies, waits for them, and re-layouts: 4.68 us -> none
    pallas_call x1 -> x2, Pallas kernels: 64.3 us -> 62.8 us  [the longest x1 60.7 us: on_device(): pl.pallas_call(whole_kernel, out_shape=(v(64, 128, 128), v(64, 1024), v(1...]
where the time goes in v3:
time: 63.8 us; the launch traced here: 63.7 us
  Pallas kernels  62.8 us (98%)
  between operations  0.82 us (1%)
    pallas_call x1, Pallas kernels, on_device(): pl.pallas_call(whole_kernel, out_shape=(v(64, 128, 128), v(64, 1024), v(1...  60.7 us
    pallas_call x1, Pallas kernels, on_device(): pl.pallas_call(finish_kernel, out_shape=(jax.ShapeDtypeStruct((64, 128, 1...  2.16 us

profile of v3, /device:TPU:1, one launch (start us, length us, event | category | flops | bytes accessed | tf_op | source)
XLA Modules:
  0.0 63.7 jit_solution(8045628679917655047)
XLA Ops:
  0.6 60.7 %whole.1 = (bf16[64,128,128]{2,1,0:T(8,128)(2,1)S(1)}, bf16[64,1024]{1,0:T(8,128)(2,1)S(1)}, bf16[16,64,128]{2,1,0:T(8,128)(2,1)S(1)}) custom-call(bf16[64,1024]{1,0:T(8,128)(2,1)} %bitcast.7, bf16[64,64]{1,0:T(8,128)(2,1)} %ws_ref.1, bf16[1024,128]{1,0:T(8,128)(2,1)} %w.1, bf16[1,128]{1,0:T(2,128)(2,1)} %bitcast.8, bf16[64,128,128]{2,1,0:T(8,128)(2,1)} %cot_hbm.1), custom_call_target="tpu_custom_call" | custom-call | tf_op jit(solution)/shard_map/whole/pallas_call | solution.py:482
  61.3 2.2 %finish.1 = (bf16[64,128,128]{2,1,0:T(8,128)(2,1)}, bf16[64,1024]{1,0:T(8,128)(2,1)}, f32[1024,128]{1,0:T(8,128)}) custom-call(bf16[64,128,128]{2,1,0:T(8,128)(2,1)S(1)} %get-tuple-element.9.pair, bf16[64,1024]{1,0:T(8,128)(2,1)S(1)} %get-tuple-element.10.grad, bf16[16,64,128]{2,1,0:T(8,128)(2,1)S(1)} %get-tuple-element.11.wall), custom_call_target="tpu_custom_call" | custom-call | tf_op jit(solution)/shard_map/finish/pallas_call | solution.py:502

commit v4 on v3

--- a/solution.py
+++ b/solution.py
@@ -85,100 +85,92 @@
     lsend[...] = acc.astype(BF).reshape(16, 16, 128)
 
 
-def scatter_start(r, q, lsend, rsend, l1, r1, sems):
-    ls, lr, rs, rr = sems
-    out = []
+def taken(ref, sem, peer):
+    remote(ref, ref, sem, sem, peer).wait_recv()
+
+
+def gone(ref, sem, peer):
+    remote(ref, ref, sem, sem, peer).wait_send()
+
+
+def to_row(p, src, dst, sems):
+    r, q = p[0], p[1]
     for d in range(1, 16):
         to = lax.rem(r + d, 16)
-        cp = remote(lsend.at[to], l1.at[r], ls.at[d], lr.at[r], (to, q))
-        cp.start()
-        out.append(cp)
+        remote(src(to), dst.at[r], sems.at[0], sems.at[1], (to, q)).start()
+
+
+def to_col(p, src, dst, sems):
+    r, q = p[0], p[1]
     for d in range(1, 8):
         to = lax.rem(q + d, 8)
-        cp = remote(rsend.at[to], r1.at[q], rs.at[d], rr.at[q], (r, to))
-        cp.start()
-        out.append(cp)
-    return out
-
-
-def wait_row(r, q, buf, recv, send):
-    for d in range(1, 16):
-        at = lax.rem(r + d, 16)
-        remote(buf.at[at], buf.at[at], send.at[d], recv.at[at], (at, q)).wait_recv()
-
-
-def wait_col(r, q, buf, recv, send):
-    for d in range(1, 8):
-        at = lax.rem(q + d, 8)
-        remote(buf.at[at], buf.at[at], send.at[d], recv.at[at], (r, at)).wait_recv()
+        remote(src(to), dst.at[q], sems.at[0], sems.at[1], (r, to)).start()
 
 
 class Sends:
     def __init__(self, buf, send, recv):
-        self.buf, self.send, self.recv, self.n, self.all = buf, send, recv, 0, []
-
-    def start(self, slot, to):
+        self.buf, self.send, self.recv = buf, send, recv
+
+    def start(self, slot, to, at):
         ref = self.buf.at[:, slot]
-        cp = remote(ref, ref, self.send.at[self.n], self.recv.at[slot], to)
-        self.n += 1
-        cp.start()
-        self.all.append(cp)
-
-    def arrived(self, slot, source):
-        ref = self.buf.at[:, slot]
-        remote(ref, ref, self.send.at[0], self.recv.at[slot], source).wait_recv()
+        remote(ref, ref, self.send.at[0], self.recv.at[at], to).start()
+
+    def arrived(self, slot, source, at):
+        taken(self.buf.at[:, slot], self.recv.at[at], source)
 
 
 def spread_left(p, sends):
     r, q, y, zh, c, x, zl = p
     over = x * 2 + 1 - zl
-    sends.start(q, (r, over))
+    sends.start(q, (r, over), 0)
     for d in (1, 3, 2):
-        sends.start(q, (r, lax.rem(x + d, 4) * 2 + zl))
+        sends.start(q, (r, lax.rem(x + d, 4) * 2 + zl), 1)
 
     def relay():
-        sends.arrived(over, (r, over))
+        sends.arrived(over, (r, over), 0)
         for d in (1, 3, 2):
-            sends.start(over, (r, lax.rem(x + d, 4) * 2 + zl))
+            sends.start(over, (r, lax.rem(x + d, 4) * 2 + zl), 1)
 
     def rest():
-        for d in (1, 3, 2):
-            xd = lax.rem(x + d, 4)
-            sends.arrived(xd * 2 + zl, (r, xd * 2 + zl))
-            sends.arrived(xd * 2 + 1 - zl, (r, xd * 2 + zl))
-
-    return relay, rest
+        taken(sends.buf.at[:, pl.ds(0, 6)], sends.recv.at[1], (r, over))
+
+    def left():
+        gone(sends.buf.at[:, pl.ds(0, 7)], sends.send.at[0], (r, over))
+
+    return relay, rest, left
 
 
 def spread_right(p, sends):
     r, q, y, zh, c, x, zl = p
     over = row_of(y, 1 - zh, c)
     mate = row_of(y, zh, 1 - c)
-    sends.start(r, (over, q))
+    sends.start(r, (over, q), 0)
     for d in (1, 3, 2):
-        sends.start(r, (row_of(lax.rem(y + d, 4), zh, c), q))
-    sends.start(r, (mate, q))
+        sends.start(r, (row_of(lax.rem(y + d, 4), zh, c), q), d)
+    sends.start(r, (mate, q), 7)
 
     def relay():
-        sends.arrived(over, (over, q))
+        sends.arrived(over, (over, q), 0)
         for d in (1, 3, 2):
-            sends.start(over, (row_of(lax.rem(y + d, 4), zh, c), q))
-        sends.start(over, (mate, q))
+            sends.start(over, (row_of(lax.rem(y + d, 4), zh, c), q), 3 + d)
+        sends.start(over, (mate, q), 7)
 
     def pass_on():
-        for zz in (zh, 1 - zh):
-            for d in (1, 3, 2):
+        for far in range(2):
+            zz = zh if far == 0 else 1 - zh
+            for d in (3, 1, 2):
                 yd = lax.rem(y + d, 4)
                 slot = row_of(yd, zz, c)
-                sends.arrived(slot, (row_of(yd, zh, c), q))
-                sends.start(slot, (mate, q))
+                sends.arrived(slot, (row_of(yd, zh, c), q), 3 * far + 4 - d)
+                sends.start(slot, (mate, q), 7)
 
     def rest():
-        for zz in (zh, 1 - zh):
-            for d in range(4):
-                sends.arrived(row_of(lax.rem(y + d, 4), zz, 1 - c), (mate, q))
-
-    return relay, pass_on, rest
+        taken(sends.buf.at[:, pl.ds(0, 8)], sends.recv.at[7], (mate, q))
+
+    def left():
+        gone(sends.buf.at[:, pl.ds(0, 15)], sends.send.at[0], (mate, q))
+
+    return relay, pass_on, rest, left
 
 
 def natural_left(l3, l4, lt):
@@ -266,28 +258,6 @@
     steps(lo, hi, body)
 
 
-def to_row(p, src, dst, send, recv):
-    r, q = p[0], p[1]
-    out = []
-    for d in range(1, 16):
-        to = lax.rem(r + d, 16)
-        cp = remote(src(to), dst.at[r], send.at[d], recv.at[r], (to, q))
-        cp.start()
-        out.append(cp)
-    return out
-
-
-def to_col(p, src, dst, send, recv):
-    r, q = p[0], p[1]
-    out = []
-    for d in range(1, 8):
-        to = lax.rem(q + d, 8)
-        cp = remote(src(to), dst.at[q], send.at[d], recv.at[q], (r, to))
-        cp.start()
-        out.append(cp)
-    return out
-
-
 def summed(buf, n):
     acc = buf[0].astype(F32)
     for k in range(1, n):
@@ -297,17 +267,17 @@
 
 def whole_kernel(
     x, ws_ref, w, bias, cot_hbm, pair, grad, wall,
-    xt, xs, wf, wr, wt, cot, G, O, raw, order,
+    xt, ns, xs, wf, wr, wt, cot, G, O, raw, order,
     lsend, rsend, l1, r1, l3, r3, rn, l4, lt,
     rg, rc, rcs, ry, rys, rz, r6, rin, lg, lx, l6, lin,
     wg, wgot, wsum, wc,
     cot_sem,
-    ls, lr, rs, rr, l2s, l2r, r2s, r2r,
-    cs, cr, ys, yr, xs_s, xs_r, zs, zr, lo_s, lo_r, ro_s, ro_r, w1s, w1r, w2s, w2r, w3s, w3r,
+    la, ra, l2s, l2r, r2s, r2r, cores, ys, lxsem, zs, lo, ro, w1, w2, w3,
 ):
     p = place()
     r, q, y, zh, c, xx, zl = p
     mate = (row_of(y, zh, 1 - c), q)
+    beside = (r, lax.rem(q + 1, 8))
     greet(r, q)
     cot_copy = pltpu.make_async_copy(cot_hbm, cot, cot_sem.at[0])
     cot_copy.start()
@@ -318,7 +288,8 @@
     l1[r] = lsend[r]
     r1[q] = rsend[q]
     greeted()
-    sent = scatter_start(r, q, lsend, rsend, l1, r1, (ls, lr, rs, rr))
+    to_col(p, lambda to: rsend.at[to], r1, ra)
+    to_row(p, lambda to: lsend.at[to], l1, la)
     wf[...] = w[...].astype(F32)
     for e in range(32):
         wr[e * 32 : (e + 1) * 32, :] = wf[pl.ds(e, 32, stride=32), :].astype(BF)
@@ -330,14 +301,14 @@
     left_order, right_order = swapped(16, 16), swapped(8, 32)
     cot_copy.wait()
     grad_outer(cot, wr, G, 0, 2)
-    wait_col(r, q, r1, rr, rs)
+    taken(r1.at[pl.ds(0, 7)], ra.at[1], beside)
     r3[:, r] = dot(right_order, r1[...].reshape(256, 128)).reshape(32, 8, 128).astype(BF)
     rsends = Sends(r3, r2s, r2r)
-    rrelay, rpass, rrest = spread_right(p, rsends)
-    wait_row(r, q, l1, lr, ls)
+    rrelay, rpass, rrest, rleft = spread_right(p, rsends)
+    taken(l1.at[pl.ds(0, 15)], la.at[1], mate)
     l3[:, q] = dot(left_order, l1[...].reshape(256, 128)).astype(BF).reshape(16, 16, 128)
     lsends = Sends(l3, l2s, l2r)
-    lrelay, lrest = spread_left(p, lsends)
+    lrelay, lrest, lleft = spread_left(p, lsends)
     grad_outer(cot, wr, G, 2, 3)
     rrelay()
     lrelay()
@@ -349,39 +320,29 @@
     def put_right(e, v):
         rg[e] = v.reshape(8, 2, 8, 128).astype(BF)
 
-    core = []
     for half in range(2):
         right_gradient(G, l4, put_right, half, half + 1)
         es = pl.ds(half * 16, 16)
-        cp = remote(rg.at[es, :, 1 - c], rc.at[es], cs.at[half], cr.at[half], mate)
-        cp.start()
-        core.append(cp)
+        remote(rg.at[es, :, 1 - c], rc.at[es], cores.at[0], cores.at[1], mate).start()
     rrest()
     for e in range(32):
         rn[e] = r3[e].reshape(128, 128)
 
-    ycp, xcp, one = [], [], []
     outer_product(lt, rn, O, 0, chunk[0])
     for at in range(4):
         if at < 3:
             outer_product(lt, rn, O, at + 1, chunk[at + 1])
         if at == 0:
-            for cp in core:
-                cp.wait_recv()
+            taken(rc, cores.at[1], mate)
             for e in range(32):
                 rcs[e] = (rg[e, :, c].astype(F32) + rc[e].astype(F32)).astype(BF)
             for d in (1, 3, 2):
                 to = lax.rem(y + d, 4)
-                cp = remote(rcs.at[:, pl.ds(to * 2, 2)], ry.at[d - 1], ys.at[d - 1], yr.at[d - 1], (row_of(to, zh, c), q))
-                cp.start()
-                ycp.append(cp)
+                remote(rcs.at[:, pl.ds(to * 2, 2)], ry.at[d - 1], ys.at[0], ys.at[1], (row_of(to, zh, c), q)).start()
         wg[4 * at : 4 * at + 4] = weight_gradient(O, cot, at).astype(BF).reshape(4, 64, 128)
         for k in range(4 if at < 3 else 3):
             piece = k if at < 3 else lax.rem(zh * 2 + c + k + 1, 4)
-            sem = w1s.at[4 * at + k]
-            cp = remote(wg.at[4 * at + piece], wgot.at[r], sem, w1r.at[r], (chunk[at] * 4 + piece, q))
-            cp.start()
-            sent.append(cp)
+            remote(wg.at[4 * at + piece], wgot.at[r], w1.at[0], w1.at[1], (chunk[at] * 4 + piece, q)).start()
     wgot[r] = wg[12 + zh * 2 + c]
 
     def put_left(m):
@@ -390,11 +351,8 @@
         rows = pl.ds(m * 4, 4)
         for d in (4, 5, 3, 6, 2, 7, 1):
             to = lax.rem(q + d, 8)
-            at = (d - 1) * 4 + m
             src = lg.at[rows, pl.ds(pl.multiple_of(to * 16, 16), 16), :]
-            cp = remote(src, lx.at[q, rows], xs_s.at[at], xs_r.at[q * 4 + m], (r, to))
-            cp.start()
-            sent.append(cp)
+            remote(src, lx.at[q, rows], lxsem.at[0], lxsem.at[1], (r, to)).start()
 
     for m in range(4):
         block = left_gradient(G, rn, m).astype(BF)
@@ -402,72 +360,82 @@
             put_left(m - 1)
         raw[m * 512 : (m + 1) * 512, :] = block
         if m == 0:
-            for cp in ycp:
-                cp.wait_recv()
+            taken(ry, ys.at[1], mate)
             for e in range(32):
                 own = rcs[e, pl.ds(y * 2, 2)].astype(F32)
                 for d in range(3):
                     own = own + ry[d, e].astype(F32)
                 rys[e] = own.astype(BF)
-            rzc = remote(rys.at[:, 1 - zh], rz, zs.at[0], zr.at[0], (row_of(y, 1 - zh, c), q))
+            rzc = remote(rys.at[:, 1 - zh], rz, zs.at[0], zs.at[1], (row_of(y, 1 - zh, c), q))
             rzc.start()
-            one.append(rzc)
+        if m == 2:
+            taken(wgot.at[pl.ds(0, 15)], w1.at[1], mate)
+            wsum[...] = summed(wgot, 16).astype(BF)
+            wc[q] = wsum[...]
+            to_col(p, lambda to: wsum, wc, w2)
     put_left(3)
-    wait_row(r, q, wgot, w1r, w1s)
-    wsum[...] = summed(wgot, 16).astype(BF)
-    wc[q] = wsum[...]
-    sent += to_col(p, lambda to: wsum, wc, w2s, w2r)
     rzc.wait_recv()
     five = rys[:, zh].astype(F32) + rz[...].astype(F32)
     r6[...] = dot(swapped(32, 8), five.reshape(256, 128).astype(BF)).astype(BF).reshape(8, 32, 128)
     rin[q] = r6[q]
-    sent += to_col(p, lambda to: r6.at[to], rin, ro_s, ro_r)
+    to_col(p, lambda to: r6.at[to], rin, ro)
     order2 = swapped(16, 16)
 
     pair_update(O, wt, bias, pair, 0, 4)
 
-    wait_col(r, q, wc, w2r, w2s)
+    taken(wc.at[pl.ds(0, 7)], w2.at[1], beside)
     wall[r] = summed(wc, 8).astype(BF)
-    sent += to_row(p, lambda to: wall.at[r], wall, w3s, w3r)
-    for d in range(1, 8):
-        at = lax.rem(q + d, 8)
-        for m in range(4):
-            ref = lx.at[at, pl.ds(m * 4, 4)]
-            remote(ref, ref, xs_s.at[0], xs_r.at[at * 4 + m], (r, at)).wait_recv()
+    to_row(p, lambda to: wall.at[r], wall, w3)
+    taken(lx.at[pl.ds(0, 7)], lxsem.at[1], beside)
     lx[q] = lg[:, pl.ds(pl.multiple_of(q * 16, 16), 16), :]
     five = summed(lx, 8).astype(BF)
     l6[...] = dot(order2, five.reshape(256, 128)).astype(BF).reshape(16, 16, 128)
     lin[r] = l6[r]
-    sent += to_row(p, lambda to: l6.at[to], lin, lo_s, lo_r)
-    wait_row(r, q, wall, w3r, w3s)
-    wait_col(r, q, rin, ro_r, ro_s)
-    wait_row(r, q, lin, lo_r, lo_s)
+    to_row(p, lambda to: l6.at[to], lin, lo)
+    gone(rsend.at[pl.ds(0, 7)], ra.at[0], beside)
+    gone(lsend.at[pl.ds(0, 15)], la.at[0], mate)
+    rleft()
+    lleft()
+    gone(rc, cores.at[0], mate)
+    gone(ry, ys.at[0], mate)
+    rzc.wait_send()
+    gone(wgot.at[pl.ds(0, 15)], w1.at[0], mate)
+    gone(lx.at[pl.ds(0, 7)], lxsem.at[0], beside)
+    gone(wc.at[pl.ds(0, 7)], w2.at[0], beside)
+    gone(rin.at[pl.ds(0, 7)], ro.at[0], beside)
+    taken(rin.at[pl.ds(0, 7)], ro.at[1], beside)
+    right = ws[:, 32:].astype(BF)
+    for k in range(8):
+        ns[:, k * 128 : (k + 1) * 128] = dot(right, rin[k])
+    taken(lin.at[pl.ds(0, 15)], lo.at[1], mate)
     flat = lin[...].reshape(256, 128)
     for t in range(4):
         xs[pl.ds(t, 256, stride=4), :] = dnt(flat, widened(ws, t))
-    right = ws[:, 32:].astype(BF)
     for k in range(8):
         cols = slice(k * 128, (k + 1) * 128)
-        ng = dot(right, rin[k]) + xs[cols, :].T
+        ng = ns[:, cols] + xs[cols, :].T
         xh = xt[:, cols]
         first = jnp.mean(ng, axis=0, keepdims=True)
         second = jnp.mean(ng * xh, axis=0, keepdims=True)
         grad[:, cols] = (rstd[:, cols] * (ng - first - xh * second)).astype(BF)
-    for cp in sent + rsends.all + lsends.all + core + ycp + xcp + one:
-        cp.wait_send()
-
-
-def finish_kernel(pair, grad, wall, pair_out, grad_out, wout, wf, sems):
+    taken(wall.at[pl.ds(0, 15)], w3.at[1], mate)
+    gone(lin.at[pl.ds(0, 15)], lo.at[0], mate)
+    gone(wall.at[pl.ds(0, 15)], w3.at[0], mate)
+
+
+def finish_kernel(pair, grad, wall, pair_out, grad_out, wout, wf, wo, sems):
     cps = [
         pltpu.make_async_copy(pair, pair_out, sems.at[0]),
         pltpu.make_async_copy(grad, grad_out, sems.at[1]),
+        pltpu.make_async_copy(wo, wout, sems.at[2]),
     ]
-    for cp in cps:
-        cp.start()
+    cps[0].start()
+    cps[1].start()
     for k in range(16):
         wf[k * 64 : (k + 1) * 64, :] = wall[k].astype(F32)
     for k in range(32):
-        wout[k * 32 : (k + 1) * 32, :] = wf[pl.ds(k, 32, stride=32), :]
+        wo[k * 32 : (k + 1) * 32, :] = wf[pl.ds(k, 32, stride=32), :]
+    cps[2].start()
     for cp in cps:
         cp.wait()
 
@@ -484,7 +452,7 @@
         out_shape=(v(64, 128, 128), v(64, 1024), v(16, 64, 128)),
         in_specs=[VM, VM, VM, VM, ANY],
         out_specs=(VM, VM, VM),
-        scratch_shapes=[f(64, 1024), f(1024, 64), f(1024, 128), v(1024, 128), v(128, 1024), v(64, 128, 128)]
+        scratch_shapes=[f(64, 1024), f(64, 1024), f(1024, 64), f(1024, 128), v(1024, 128), v(128, 1024), v(64, 128, 128)]
         + [v(32, 2048, 128), v(32, 2048, 128), v(2048, 128), v(128, 128)]
         + [v(16, 16, 128), v(8, 32, 128), v(16, 16, 128), v(8, 32, 128), v(16, 8, 16, 128), v(32, 16, 8, 128), v(32, 128, 128)]
         + [v(16, 128, 128), v(2048, 128)]
@@ -493,9 +461,8 @@
         + [v(16, 128, 128), v(8, 16, 16, 128), v(16, 16, 128), v(16, 16, 128)]
         + [v(16, 64, 128), v(16, 64, 128), v(64, 128), v(8, 64, 128)]
         + [DMA((1,))]
-        + [DMA((16,)), DMA((16,)), DMA((8,)), DMA((8,)), DMA((7,)), DMA((8,)), DMA((15,)), DMA((16,))]
-        + [DMA((2,)), DMA((2,)), DMA((3,)), DMA((3,)), DMA((28,)), DMA((32,)), DMA((1,)), DMA((1,))]
-        + [DMA((16,)), DMA((16,)), DMA((8,)), DMA((8,)), DMA((16,)), DMA((16,)), DMA((8,)), DMA((8,)), DMA((16,)), DMA((16,))],
+        + [DMA((2,)), DMA((2,)), DMA((1,)), DMA((2,)), DMA((1,)), DMA((8,))]
+        + [DMA((2,))] * 9,
         compiler_params=pltpu.CompilerParams(vmem_limit_bytes=54 << 20, collective_id=0, has_side_effects=True),
         name="whole",
     )(x[0].T, ws, w, bias.reshape(1, 128), cot)
@@ -507,8 +474,8 @@
             jax.ShapeDtypeStruct((1024, 128), F32),
         ),
         in_specs=[VM, VM, VM],
-        out_specs=(ANY, ANY, VM),
-        scratch_shapes=[f(1024, 128), DMA((2,))],
+        out_specs=(ANY, ANY, ANY),
+        scratch_shapes=[f(1024, 128), f(1024, 128), DMA((3,))],
         compiler_params=pltpu.CompilerParams(vmem_limit_bytes=8 << 20),
         name="finish",
     )(pair, grad, wall)

time: 63.8 us -> 60.3 us (0.945)
  Pallas kernels: 62.8 us -> 59.4 us
    pallas_call x1, Pallas kernels: 60.7 us -> 57.8 us  [on_device(): pl.pallas_call(whole_kernel, out_shape=(v(64, 128, 128), v(64, 1024), v(1...]
where the time goes in v4:
time: 60.3 us; the launch traced here: 60.2 us
  Pallas kernels  59.4 us (99%)
  between operations  0.82 us (1%)
    pallas_call x1, Pallas kernels, on_device(): pl.pallas_call(whole_kernel, out_shape=(v(64, 128, 128), v(64, 1024), v(1...  57.8 us
    pallas_call x1, Pallas kernels, on_device(): pl.pallas_call(finish_kernel, out_shape=(jax.ShapeDtypeStruct((64, 128, 1...  1.55 us

profile of v4, /device:TPU:1, one launch (start us, length us, event | category | flops | bytes accessed | tf_op | source)
XLA Modules:
  0.0 60.2 jit_solution(13289195080729007777)
XLA Ops:
  0.6 57.8 %whole.1 = (bf16[64,128,128]{2,1,0:T(8,128)(2,1)S(1)}, bf16[64,1024]{1,0:T(8,128)(2,1)S(1)}, bf16[16,64,128]{2,1,0:T(8,128)(2,1)S(1)}) custom-call(bf16[64,1024]{1,0:T(8,128)(2,1)} %bitcast.7, bf16[64,64]{1,0:T(8,128)(2,1)} %ws_ref.1, bf16[1024,128]{1,0:T(8,128)(2,1)} %w.1, bf16[1,128]{1,0:T(2,128)(2,1)} %bitcast.8, bf16[64,128,128]{2,1,0:T(8,128)(2,1)} %cot_hbm.1), custom_call_target="tpu_custom_call" | custom-call | tf_op jit(solution)/shard_map/whole/pallas_call | solution.py:450
  58.5 1.6 %finish.1 = (bf16[64,128,128]{2,1,0:T(8,128)(2,1)}, bf16[64,1024]{1,0:T(8,128)(2,1)}, f32[1024,128]{1,0:T(8,128)}) custom-call(bf16[64,128,128]{2,1,0:T(8,128)(2,1)S(1)} %get-tuple-element.9.pair, bf16[64,1024]{1,0:T(8,128)(2,1)S(1)} %get-tuple-element.10.grad, bf16[16,64,128]{2,1,0:T(8,128)(2,1)S(1)} %get-tuple-element.11.wall), custom_call_target="tpu_custom_call" | custom-call | tf_op jit(solution)/shard_map/finish/pallas_call | solution.py:469

commit v5 on v4

--- a/solution.py
+++ b/solution.py
@@ -310,8 +310,8 @@
     lsends = Sends(l3, l2s, l2r)
     lrelay, lrest, lleft = spread_left(p, lsends)
     grad_outer(cot, wr, G, 2, 3)
+    lrelay()
     rrelay()
-    lrelay()
     grad_outer(cot, wr, G, 3, 4)
     lrest()
     natural_left(l3, l4, lt)
@@ -359,33 +359,32 @@
         if m > 0:
             put_left(m - 1)
         raw[m * 512 : (m + 1) * 512, :] = block
-        if m == 0:
-            taken(ry, ys.at[1], mate)
-            for e in range(32):
-                own = rcs[e, pl.ds(y * 2, 2)].astype(F32)
-                for d in range(3):
-                    own = own + ry[d, e].astype(F32)
-                rys[e] = own.astype(BF)
-            rzc = remote(rys.at[:, 1 - zh], rz, zs.at[0], zs.at[1], (row_of(y, 1 - zh, c), q))
-            rzc.start()
         if m == 2:
             taken(wgot.at[pl.ds(0, 15)], w1.at[1], mate)
             wsum[...] = summed(wgot, 16).astype(BF)
             wc[q] = wsum[...]
             to_col(p, lambda to: wsum, wc, w2)
     put_left(3)
+    taken(ry, ys.at[1], mate)
+    for e in range(32):
+        own = rcs[e, pl.ds(y * 2, 2)].astype(F32)
+        for d in range(3):
+            own = own + ry[d, e].astype(F32)
+        rys[e] = own.astype(BF)
+    rzc = remote(rys.at[:, 1 - zh], rz, zs.at[0], zs.at[1], (row_of(y, 1 - zh, c), q))
+    rzc.start()
+    order2 = swapped(16, 16)
+
+    pair_update(O, wt, bias, pair, 0, 4)
+
+    taken(wc.at[pl.ds(0, 7)], w2.at[1], beside)
+    wall[r] = summed(wc, 8).astype(BF)
+    to_row(p, lambda to: wall.at[r], wall, w3)
     rzc.wait_recv()
     five = rys[:, zh].astype(F32) + rz[...].astype(F32)
     r6[...] = dot(swapped(32, 8), five.reshape(256, 128).astype(BF)).astype(BF).reshape(8, 32, 128)
     rin[q] = r6[q]
     to_col(p, lambda to: r6.at[to], rin, ro)
-    order2 = swapped(16, 16)
-
-    pair_update(O, wt, bias, pair, 0, 4)
-
-    taken(wc.at[pl.ds(0, 7)], w2.at[1], beside)
-    wall[r] = summed(wc, 8).astype(BF)
-    to_row(p, lambda to: wall.at[r], wall, w3)
     taken(lx.at[pl.ds(0, 7)], lxsem.at[1], beside)
     lx[q] = lg[:, pl.ds(pl.multiple_of(q * 16, 16), 16), :]
     five = summed(lx, 8).astype(BF)

time: 60.3 us -> 60.8 us (level)
  no operation moved by 1% of the time
where the time goes in v5:
time: 60.8 us; the launch traced here: 60.7 us
  Pallas kernels  59.9 us (99%)
  between operations  0.82 us (1%)
    pallas_call x1, Pallas kernels, on_device(): pl.pallas_call(whole_kernel, out_shape=(v(64, 128, 128), v(64, 1024), v(1...  58.3 us
    pallas_call x1, Pallas kernels, on_device(): pl.pallas_call(finish_kernel, out_shape=(jax.ShapeDtypeStruct((64, 128, 1...  1.55 us

profile of v5, /device:TPU:1, one launch (start us, length us, event | category | flops | bytes accessed | tf_op | source)
XLA Modules:
  0.0 60.7 jit_solution(8850474322563617554)
XLA Ops:
  0.6 58.3 %whole.1 = (bf16[64,128,128]{2,1,0:T(8,128)(2,1)S(1)}, bf16[64,1024]{1,0:T(8,128)(2,1)S(1)}, bf16[16,64,128]{2,1,0:T(8,128)(2,1)S(1)}) custom-call(bf16[64,1024]{1,0:T(8,128)(2,1)} %bitcast.7, bf16[64,64]{1,0:T(8,128)(2,1)} %ws_ref.1, bf16[1024,128]{1,0:T(8,128)(2,1)} %w.1, bf16[1,128]{1,0:T(2,128)(2,1)} %bitcast.8, bf16[64,128,128]{2,1,0:T(8,128)(2,1)} %cot_hbm.1), custom_call_target="tpu_custom_call" | custom-call | tf_op jit(solution)/shard_map/whole/pallas_call | solution.py:449
  58.9 1.6 %finish.1 = (bf16[64,128,128]{2,1,0:T(8,128)(2,1)}, bf16[64,1024]{1,0:T(8,128)(2,1)}, f32[1024,128]{1,0:T(8,128)}) custom-call(bf16[64,128,128]{2,1,0:T(8,128)(2,1)S(1)} %get-tuple-element.9.pair, bf16[64,1024]{1,0:T(8,128)(2,1)S(1)} %get-tuple-element.10.grad, bf16[16,64,128]{2,1,0:T(8,128)(2,1)S(1)} %get-tuple-element.11.wall), custom_call_target="tpu_custom_call" | custom-call | tf_op jit(solution)/shard_map/finish/pallas_call | solution.py:468

commit v6 on v4

--- a/solution.py
+++ b/solution.py
@@ -310,8 +310,8 @@
     lsends = Sends(l3, l2s, l2r)
     lrelay, lrest, lleft = spread_left(p, lsends)
     grad_outer(cot, wr, G, 2, 3)
+    lrelay()
     rrelay()
-    lrelay()
     grad_outer(cot, wr, G, 3, 4)
     lrest()
     natural_left(l3, l4, lt)

time: 60.3 us -> 60.6 us (level)
  no operation moved by 1% of the time
where the time goes in v6:
time: 60.6 us; the launch traced here: 60.4 us
  Pallas kernels  59.6 us (98%)
  between operations  0.82 us (1%)
    pallas_call x1, Pallas kernels, on_device(): pl.pallas_call(whole_kernel, out_shape=(v(64, 128, 128), v(64, 1024), v(1...  58.1 us
    pallas_call x1, Pallas kernels, on_device(): pl.pallas_call(finish_kernel, out_shape=(jax.ShapeDtypeStruct((64, 128, 1...  1.55 us

profile of v6, /device:TPU:1, one launch (start us, length us, event | category | flops | bytes accessed | tf_op | source)
XLA Modules:
  0.0 60.4 jit_solution(1115353881909162460)
XLA Ops:
  0.6 58.1 %whole.1 = (bf16[64,128,128]{2,1,0:T(8,128)(2,1)S(1)}, bf16[64,1024]{1,0:T(8,128)(2,1)S(1)}, bf16[16,64,128]{2,1,0:T(8,128)(2,1)S(1)}) custom-call(bf16[64,1024]{1,0:T(8,128)(2,1)} %bitcast.7, bf16[64,64]{1,0:T(8,128)(2,1)} %ws_ref.1, bf16[1024,128]{1,0:T(8,128)(2,1)} %w.1, bf16[1,128]{1,0:T(2,128)(2,1)} %bitcast.8, bf16[64,128,128]{2,1,0:T(8,128)(2,1)} %cot_hbm.1), custom_call_target="tpu_custom_call" | custom-call | tf_op jit(solution)/shard_map/whole/pallas_call | solution.py:450
  58.7 1.6 %finish.1 = (bf16[64,128,128]{2,1,0:T(8,128)(2,1)}, bf16[64,1024]{1,0:T(8,128)(2,1)}, f32[1024,128]{1,0:T(8,128)}) custom-call(bf16[64,128,128]{2,1,0:T(8,128)(2,1)S(1)} %get-tuple-element.9.pair, bf16[64,1024]{1,0:T(8,128)(2,1)S(1)} %get-tuple-element.10.grad, bf16[16,64,128]{2,1,0:T(8,128)(2,1)S(1)} %get-tuple-element.11.wall), custom_call_target="tpu_custom_call" | custom-call | tf_op jit(solution)/shard_map/finish/pallas_call | solution.py:469
